TPU v7x, 32 devices: a whole 2x2x4 slice. The times are simulated.
32 devices in a mesh: batch: 4 (over x, core), seq: 8 (over z, y).
Axes of the slice: x: 2, y: 2, z: 4, core: 2. Of those that a mesh axis runs over, the one named last changes fastest.
Arguments:
- signal: bfloat16 [4, 2048, 256], P('batch', 'seq'), may hold values from -0.3125 to 0.3125
- grad_out: bfloat16 [4, 2048, 256], P('batch', 'seq'), may hold values from -6 to 6
- filter_taps: float32 [2048, 256], P('seq'), may hold values from -0.3125 to 0.3125
- skip_gain: float32 [256], replicated, may hold values from 0.5 to 2
Outputs:
- input_grad: bfloat16 [4, 2048, 256], P('batch', 'seq')
- filter_grad: float32 [2048, 256], P('seq')
All inputs are finite; a program needn't handle non-finite values.
Results may differ from a plain program's by a relative error of at most 0.001.
Values sent between devices are 32-bit elements; how exact they have to be, the bound alone decides.
A program may use at most 64 MiB of HBM per device.

v0:
```python
import functools
import math

import jax
import jax.numpy as jnp
import numpy as np
from jax import lax
from jax.experimental import pallas as pl
from jax.experimental.pallas import tpu as pltpu
from jax.sharding import PartitionSpec as P

MESH = pl.DeviceIdType.MESH
F32 = jnp.float32
BF16 = jnp.bfloat16
GRAD, TAPS, SIGNAL, INPUT, FILTER, FORWARD = range(6)


def weighted(terms):
    total = None
    for factor, array in terms:
        if array is None or abs(factor) < 1e-12:
            continue
        if total is None:
            if abs(factor - 1.0) < 1e-12:
                total = array
            else:
                total = array * factor
        elif abs(factor - 1.0) < 1e-12:
            total = total + array
        elif abs(factor + 1.0) < 1e-12:
            total = total - array
        else:
            total = total + array * factor
    return total


def added(left, right):
    return weighted([(1.0, left), (1.0, right)])


def subtracted(left, right):
    return weighted([(1.0, left), (-1.0, right)])


def turn(real, imag, cos_turn, sin_turn):
    if imag is None:
        return real * cos_turn, -(real * sin_turn)
    return real * cos_turn + imag * sin_turn, imag * cos_turn - real * sin_turn


def coarse_forward(blocks):
    count = len(blocks)
    result = [None] * (count + 1)
    for k in range(count // 2 + 1):
        sums = []
        for parity in (0, 1):
            angles = [(math.pi * ((s * k) % (2 * count)) / count, s) for s in range(parity, count, 2)]
            sums.append(
                (
                    weighted([(math.cos(a), blocks[s]) for a, s in angles]),
                    weighted([(-math.sin(a), blocks[s]) for a, s in angles]),
                )
            )
        (even_re, even_im), (odd_re, odd_im) = sums
        result[k] = (added(even_re, odd_re), added(even_im, odd_im))
        if k != count - k:
            result[count - k] = (subtracted(even_re, odd_re), subtracted(odd_im, even_im))
    return result


def coarse_inverse(terms, scale):
    count = len(terms) - 1
    pairs = []
    for k in range(count // 2 + 1):
        weight = scale if k == 0 else 2.0 * scale
        real, imag = terms[k]
        if k == count - k:
            pairs.append((weight, real, imag, real, imag))
        else:
            other_re, other_im = terms[count - k]
            pairs.append((weight, real + other_re, imag - other_im, real - other_re, imag + other_im))
    blocks = []
    for s in range(count):
        parts = []
        for k, (weight, even_re, even_im, odd_re, odd_im) in enumerate(pairs):
            angle = math.pi * ((s * k) % (2 * count)) / count
            parts.append((weight * math.cos(angle) * (1 if abs(math.cos(angle)) > 1e-9 else 0), odd_re if s % 2 else even_re))
            parts.append((weight * math.sin(angle) * (1 if abs(math.sin(angle)) > 1e-9 else 0), odd_im if s % 2 else even_im))
        blocks.append(weighted(parts))
    return blocks


def fused_kernel(
    groups, seqs,
    signal_hbm, grad_hbm, tap_hbm, skip_hbm, high_hbm, low_hbm, cos_hbm, sin_hbm,
    input_hbm, filter_hbm,
    signal_ref, grad_ref, tap_ref, skip_ref, high_ref, low_ref, cos_ref, sin_ref,
    grad_out_buf, signal_out_buf, tap_out_buf, grad_in, signal_in, tap_in,
    input_out, filter_out, input_in, filter_in,
    tap_rows, tap_spec, grad_rows, grad_spec, signal_rows, signal_spec, input_rows, filter_rows, filter_spec,
    input_ref, filter_ref, send_sems, recv_sems, load_sems,
):
    count = groups * seqs
    coarse = seqs + 1
    own, rows = grad_in.shape[1:]
    channels = count * own
    group, seq = lax.axis_index("batch"), lax.axis_index("seq")
    me = group * seqs + seq
    scale = 1.0 / (2 * seqs * rows)
    re, im = pl.ds(0, rows), pl.ds(rows, rows)

    parity, pair = lax.rem(group, 2), lax.div(group, 2)
    half_seqs, half_groups = seqs // 2, groups // 2
    upper, inner = lax.div(seq, half_seqs), lax.rem(seq, half_seqs)

    def load(index, source, target):
        return pltpu.make_async_copy(source, target, load_sems.at[index])

    loads = [
        load(index, source, target)
        for index, (source, target) in enumerate(
            (
                (grad_hbm, grad_ref), (tap_hbm, tap_ref), (signal_hbm, signal_ref),
                (cos_hbm, cos_ref), (sin_hbm, sin_ref), (high_hbm, high_ref),
                (low_hbm, low_ref), (skip_hbm, skip_ref),
            )
        )
    ]
    loads[GRAD].start()
    loads[TAPS].start()

    def seq_at(step):
        other = lax.rem(upper + 1 + lax.div(step, half_seqs), 2)
        return other * half_seqs + lax.rem(inner + step, half_seqs)

    def peer(step):
        to_seq = seq_at(lax.div(step, groups))
        to_group = lax.rem(group + step, groups)
        return to_group * seqs + to_seq, to_group, to_seq

    def over_peers(body, total, own_step):
        lax.fori_loop(0, own_step, body, 0, unroll=min(4, own_step))
        lax.fori_loop(own_step + 1, total, body, 0, unroll=min(3, total - own_step - 1))

    barrier = pltpu.get_barrier_semaphore()

    def greet(step, carry):
        _, to_group, to_seq = peer(step)
        pl.semaphore_signal(
            barrier, inc=1, device_id={"batch": to_group, "seq": to_seq}, device_id_type=MESH
        )
        return carry

    over_peers(greet, count, half_seqs * groups)
    for copy in loads[2:]:
        copy.start()

    def transfer(source, target, kind, to_group, to_seq):
        return pltpu.make_async_remote_copy(
            src_ref=source,
            dst_ref=target,
            send_sem=send_sems.at[kind],
            recv_sem=recv_sems.at[kind],
            device_id={"batch": to_group, "seq": to_seq},
            device_id_type=MESH,
        )

    def all_of(buffer, blocks, kind):
        _, to_group, to_seq = peer(0)
        view = buffer.at[pl.ds(0, blocks)]
        return transfer(view, view, kind, to_group, to_seq)

    loads[GRAD].wait()
    grad_out_buf[...] = grad_ref[...].astype(F32).T.reshape(count, own, rows)
    loads[TAPS].wait()
    tap_out_buf[...] = tap_ref[...].T.reshape(count, own, rows)
    pl.semaphore_wait(barrier, count - 1)

    def send_taps(step, carry):
        to_seq = seq_at(step)
        place = group * seqs + to_seq
        transfer(tap_out_buf.at[place], tap_in.at[seq], TAPS, group, to_seq).start()
        return carry

    def send_grads(step, carry):
        place, to_group, to_seq = peer(step)
        transfer(grad_out_buf.at[place], grad_in.at[me], GRAD, to_group, to_seq).start()
        return carry

    def send_signals(step, carry):
        place, to_group, to_seq = peer(step)
        transfer(signal_out_buf.at[place], signal_in.at[me], SIGNAL, to_group, to_seq).start()
        return carry

    over_peers(send_taps, seqs, half_seqs)
    over_peers(send_grads, count, half_seqs * groups)
    loads[SIGNAL].wait()
    signal_out_buf[...] = signal_ref[...].astype(F32).T.reshape(count, own, rows)
    over_peers(send_signals, count, half_seqs * groups)
    grad_in[me] = grad_out_buf[me]
    tap_in[seq] = tap_out_buf[me]
    signal_in[me] = signal_out_buf[me]

    def spread(blocks, target, first_row):
        place = pl.ds(first_row, own)
        for k, (real, imag) in enumerate(coarse_forward(blocks)):
            real, imag = turn(real, imag, cos_ref[k], sin_ref[k])
            target[k, place, re] = real
            target[k, place, im] = imag

    def fine(source, target):
        lines = source.shape[0] * source.shape[1]
        value = source[...].reshape(lines, 2 * rows)
        high = value.astype(BF16)
        low = (value - high.astype(F32)).astype(BF16)
        product = functools.partial(jnp.dot, preferred_element_type=F32)
        total = product(high, high_ref[...]) + product(low, high_ref[...]) + product(high, low_ref[...])
        target[...] = total.reshape(target.shape)

    def collect(source, first_row):
        place = pl.ds(first_row, own)
        terms = [
            turn(source[k, place, re], source[k, place, im], cos_ref[k], sin_ref[k])
            for k in range(coarse)
        ]
        return coarse_inverse(terms, scale)

    def row_of(index):
        return pl.multiple_of(index * own, own)

    for copy in loads[3:]:
        copy.wait()
    all_of(tap_in, seqs - 1, TAPS).wait_recv()
    spread([tap_in[s] for s in range(seqs)], tap_rows, 0)
    fine(tap_rows, tap_spec)
    all_of(grad_in, count - 1, GRAD).wait_recv()

    def group_at(index):
        return lax.rem(2 * pair + index, groups)

    def input_part(first):
        source, spectrum, lines = grad_rows.at[first], grad_spec.at[first], input_rows.at[first]

        def spread_grad(index, carry):
            here = group_at(2 * first + index)
            spread([grad_in[here * seqs + s] for s in range(seqs)], source, row_of(index))
            return carry

        lax.fori_loop(0, 2, spread_grad, 0)
        fine(source, spectrum)

        def multiply_taps(index, carry):
            place = pl.ds(row_of(index), own)
            for k in range(coarse):
                grad_re, grad_im = spectrum[k, place, re], spectrum[k, place, im]
                tap_re, tap_im = tap_spec[k, :, re], tap_spec[k, :, im]
                lines[k, place, re] = grad_re * tap_re + grad_im * tap_im
                lines[k, place, im] = grad_re * tap_im - grad_im * tap_re
            return carry

        lax.fori_loop(0, 2, multiply_taps, 0)
        fine(lines, lines)

        def collect_input(index, carry):
            here = group_at(2 * first + index)
            for s, block in enumerate(collect(lines, row_of(index))):
                input_out[here * seqs + s] = block
            return carry

        lax.fori_loop(0, 2, collect_input, 0)

        def send_inputs(step, carry):
            to_seq = seq_at(lax.div(step, 2))
            to_group = group_at(2 * first + lax.rem(parity + step, 2))
            place = to_group * seqs + to_seq
            transfer(input_out.at[place], input_in.at[me], INPUT, to_group, to_seq).start()
            return carry

        if first == 0:
            over_peers(send_inputs, 2 * seqs, 2 * half_seqs)
        else:
            lax.fori_loop(0, 2 * seqs, send_inputs, 0)

    for first in reversed(range(half_groups)):
        input_part(first)
    input_in[me] = input_out[me]

    all_of(signal_in, count - 1, SIGNAL).wait_recv()

    def spread_signal(index, carry):
        here = group_at(index)
        spread([signal_in[here * seqs + s] for s in range(seqs)], signal_rows, row_of(index))
        return carry

    lax.fori_loop(0, groups, spread_signal, 0)
    fine(signal_rows, signal_spec)
    for k in range(coarse):
        real, imag = None, None
        for index in range(groups):
            place = pl.ds(index * own, own)
            which, local = index // 2, pl.ds(index % 2 * own, own)
            grad_re, grad_im = grad_spec[which, k, local, re], grad_spec[which, k, local, im]
            signal_re, signal_im = signal_spec[k, place, re], signal_spec[k, place, im]
            real = added(real, grad_re * signal_re + grad_im * signal_im)
            imag = added(imag, grad_re * signal_im - grad_im * signal_re)
        filter_rows[k, :, re] = real
        filter_rows[k, :, im] = imag
    fine(filter_rows, filter_spec)
    for s, block in enumerate(collect(filter_spec, 0)):
        filter_out[s] = block

    def send_filters(step, carry):
        to_seq = seq_at(lax.div(step, half_groups))
        to_group = 2 * lax.rem(pair + step, half_groups) + parity
        place = pair * seqs + seq
        transfer(
            filter_out.at[to_seq], filter_in.at[parity, place], FILTER, to_group, to_seq
        ).start()
        return carry

    over_peers(send_filters, seqs * half_groups, half_seqs * half_groups)
    filter_in[parity, pair * seqs + seq] = filter_out[seq]

    half = count // 2
    all_of(input_in, count - 1, INPUT).wait_recv()
    gradient = input_in[...].reshape(channels, rows).T + skip_ref[...] * grad_ref[...].astype(F32)
    input_ref[...] = gradient.astype(BF16)
    input_store = load(len(loads), input_ref, input_hbm)
    input_store.start()
    all_of(filter_in.at[0], half - 1, FILTER).wait_recv()
    mine = filter_in.at[parity]
    partner = 2 * pair + 1 - parity
    forward = transfer(mine, mine, FORWARD, partner, seq)
    forward.start()
    forward.wait_recv()
    parts = [
        filter_in[which, first * seqs : (first + 1) * seqs].reshape(seqs * own, rows)
        for first in range(half_groups)
        for which in range(2)
    ]
    filter_ref[...] = jnp.concatenate(parts, axis=0).T
    filter_store = load(len(loads) + 1, filter_ref, filter_hbm)
    filter_store.start()
    for kind, buffer in ((GRAD, grad_in), (SIGNAL, signal_in), (INPUT, input_in)):
        all_of(buffer, count - 1, kind).wait_send()
    all_of(filter_in.at[0], half - 1, FILTER).wait_send()
    forward.wait_send()
    input_store.wait()
    filter_store.wait()
    all_of(tap_in, seqs - 1, TAPS).wait_send()


def fine_tables(rows):
    grid = np.arange(rows)
    angle = 2.0 * np.pi / rows * (np.outer(grid, grid) % rows)
    table = np.block([[np.cos(angle), -np.sin(angle)], [np.sin(angle), np.cos(angle)]]).astype(np.float32)
    high = table.astype(BF16)
    return high, (table - high.astype(np.float32)).astype(BF16)


def turn_tables(seqs, rows, lines):
    angle = np.pi / (seqs * rows) * np.outer(np.arange(seqs + 1), np.arange(rows))
    wide = np.broadcast_to(angle[:, None, :], (seqs + 1, lines, rows))
    return np.cos(wide).astype(np.float32), np.sin(wide).astype(np.float32)


def fused_shards(groups, seqs, signal, grad_out, filter_taps, skip_gain):
    rows, channels = filter_taps.shape
    count, coarse = groups * seqs, seqs + 1
    own = channels // count
    high, low = fine_tables(rows)
    cos_turn, sin_turn = turn_tables(seqs, rows, own)
    blocks = pltpu.VMEM((count, own, rows), F32)
    few = pltpu.VMEM((seqs, own, rows), F32)
    lines = lambda number: pltpu.VMEM((coarse, number * own, 2 * rows), F32)
    pairs = pltpu.VMEM((groups // 2, coarse, 2 * own, 2 * rows), F32)
    hbm = pl.BlockSpec(memory_space=pltpu.HBM)
    turns = pltpu.VMEM((coarse, own, rows), F32)
    table = pltpu.VMEM((2 * rows, 2 * rows), BF16)
    input_grad, filter_grad = pl.pallas_call(
        functools.partial(fused_kernel, groups, seqs),
        out_shape=(
            jax.ShapeDtypeStruct((rows, channels), BF16),
            jax.ShapeDtypeStruct((rows, channels), F32),
        ),
        in_specs=[hbm] * 8,
        out_specs=(hbm, hbm),
        scratch_shapes=[
            pltpu.VMEM((rows, channels), BF16), pltpu.VMEM((rows, channels), BF16),
            pltpu.VMEM((rows, channels), F32), pltpu.VMEM((1, channels), F32),
            table, table, turns, turns,
            blocks, blocks, blocks, blocks, blocks, few,
            blocks, few, blocks, pltpu.VMEM((2, count // 2, own, rows), F32),
            lines(1), lines(1), pairs, pairs, lines(groups), lines(groups),
            pairs, lines(1), lines(1),
            pltpu.VMEM((rows, channels), BF16), pltpu.VMEM((rows, channels), F32),
            pltpu.SemaphoreType.DMA((6,)),
            pltpu.SemaphoreType.DMA((6,)),
            pltpu.SemaphoreType.DMA((10,)),
        ],
        compiler_params=pltpu.CompilerParams(
            collective_id=0, has_side_effects=True, vmem_limit_bytes=67_043_328
        ),
    )(
        signal[0], grad_out[0], filter_taps, skip_gain[None, :],
        jnp.asarray(high), jnp.asarray(low), jnp.asarray(cos_turn), jnp.asarray(sin_turn),
    )
    return input_grad[None], filter_grad


def fits_fused(groups, seqs, signal, filter_taps):
    rows, channels = filter_taps.shape
    return (
        signal.shape[0] == 1
        and seqs % 2 == 0
        and groups % 2 == 0
        and rows % 128 == 0
        and channels % (8 * groups * seqs) == 0
    )


def angle_table(height, width, period):
    product = lax.broadcasted_iota(jnp.int32, (height, width), 0) * lax.broadcasted_iota(
        jnp.int32, (height, width), 1
    )
    return 2.0 * jnp.pi / period * (product % period).astype(jnp.float32)


def angle_of(product, period):
    return 2.0 * jnp.pi / period * (product % period).astype(jnp.float32)


def coarse_order(slot, seq_count):
    pair_index = slot // 2
    odd_slot = slot % 2
    return jnp.where(
        pair_index == 0,
        odd_slot * seq_count,
        jnp.where(odd_slot == 0, pair_index, 2 * seq_count - pair_index),
    )


def contract(form, table, operand):
    return jnp.einsum(form, table, operand, precision=lax.Precision.HIGHEST)


def forward_spectra(columns):
    seq_count = lax.axis_size("seq")
    row_count = columns.shape[0]
    part_rows = row_count // seq_count
    period_len = 2 * row_count * seq_count
    spread = lax.all_to_all(
        columns.reshape(1, row_count, columns.shape[1]),
        "seq",
        split_axis=1,
        concat_axis=0,
        tiled=True,
    )
    slot_grid = lax.broadcasted_iota(jnp.int32, (2 * seq_count, seq_count), 0)
    source_grid = lax.broadcasted_iota(jnp.int32, (2 * seq_count, seq_count), 1)
    first_table = angle_of(coarse_order(slot_grid, seq_count) * source_grid, 2 * seq_count)
    cos_first = jnp.cos(first_table)
    sin_first = jnp.sin(first_table)
    half_width = spread.shape[2] // 2
    real_in = spread[:, :, :half_width]
    imag_in = spread[:, :, half_width:]
    real_part = contract("ks,srw->krw", cos_first, real_in) + contract(
        "ks,srw->krw", sin_first, imag_in
    )
    imag_part = contract("ks,srw->krw", cos_first, imag_in) - contract(
        "ks,srw->krw", sin_first, real_in
    )
    global_row = lax.axis_index("seq") * part_rows + lax.broadcasted_iota(
        jnp.int32, (2 * seq_count, part_rows), 1
    )
    coarse = coarse_order(lax.broadcasted_iota(jnp.int32, (2 * seq_count, part_rows), 0), seq_count)
    phases = angle_of(global_row * coarse, period_len)
    cos_turn = jnp.cos(phases)[:, :, None]
    sin_turn = jnp.sin(phases)[:, :, None]
    rotated = jnp.stack(
        [real_part * cos_turn + imag_part * sin_turn, imag_part * cos_turn - real_part * sin_turn]
    )
    inner_table = angle_table(row_count, row_count, row_count)
    cos_inner = jnp.cos(inner_table)
    sin_inner = jnp.sin(inner_table)
    pieces = lax.all_to_all(rotated, "seq", split_axis=1, concat_axis=2, tiled=True)
    real_sum = contract("qr,krw->kqw", cos_inner, pieces[0]) + contract(
        "qr,krw->kqw", sin_inner, pieces[1]
    )
    imag_sum = contract("qr,krw->kqw", cos_inner, pieces[1]) - contract(
        "qr,krw->kqw", sin_inner, pieces[0]
    )
    return jnp.stack([real_sum, imag_sum])


def split_pairs(packed):
    reversed_q = packed[:, :, ::-1]
    zero_row = jnp.roll(reversed_q[:, 0], 1, axis=1)
    own_pair = jnp.stack([zero_row, reversed_q[:, 1]], axis=1)
    partner = jnp.where(lax.axis_index("seq") == 0, own_pair, reversed_q[:, ::-1])
    first = jnp.stack([0.5 * (packed[0] + partner[0]), 0.5 * (packed[1] - partner[1])])
    second = jnp.stack([0.5 * (packed[1] + partner[1]), 0.5 * (partner[0] - packed[0])])
    return (first, second)


def inverse_rows(spectra):
    seq_count = lax.axis_size("seq")
    row_count = spectra.shape[2]
    period_len = 2 * row_count * seq_count
    inner_table = angle_table(row_count, row_count, row_count)
    cos_inner = jnp.cos(inner_table)
    sin_inner = jnp.sin(inner_table)
    real_sum = contract("qr,krw->kqw", cos_inner, spectra[0]) - contract(
        "qr,krw->kqw", sin_inner, spectra[1]
    )
    imag_sum = contract("qr,krw->kqw", cos_inner, spectra[1]) + contract(
        "qr,krw->kqw", sin_inner, spectra[0]
    )
    coarse = coarse_order(
        2 * lax.axis_index("seq") + lax.broadcasted_iota(jnp.int32, (2, row_count), 0), seq_count
    )
    position = lax.broadcasted_iota(jnp.int32, (2, row_count), 1)
    phases = angle_of(position * coarse, period_len)
    cos_turn = jnp.cos(phases)[:, :, None]
    sin_turn = jnp.sin(phases)[:, :, None]
    rotated = jnp.stack(
        [real_sum * cos_turn - imag_sum * sin_turn, real_sum * sin_turn + imag_sum * cos_turn]
    )
    target_grid = lax.broadcasted_iota(jnp.int32, (seq_count, 2 * seq_count), 0)
    slot_grid = lax.broadcasted_iota(jnp.int32, (seq_count, 2 * seq_count), 1)
    last_table = angle_of(target_grid * coarse_order(slot_grid, seq_count), 2 * seq_count)
    cos_last = jnp.cos(last_table)
    sin_last = jnp.sin(last_table)
    pieces = lax.all_to_all(rotated, "seq", split_axis=2, concat_axis=1, tiled=True)
    value = contract("sk,krw->srw", cos_last, pieces[0]) - contract(
        "sk,krw->srw", sin_last, pieces[1]
    )
    other = contract("sk,krw->srw", sin_last, pieces[0]) + contract(
        "sk,krw->srw", cos_last, pieces[1]
    )
    gathered = (value / period_len, other / period_len)
    gathered = jnp.concatenate([gathered[0], gathered[1]], axis=2)
    home_rows = lax.all_to_all(gathered, "seq", split_axis=0, concat_axis=1, tiled=True)
    return home_rows.reshape(row_count, home_rows.shape[2])


def invert_all(spectra):
    half_width = spectra.shape[3] // 2
    joined = jnp.stack(
        [
            spectra[0, :, :, :half_width] - spectra[1, :, :, half_width:],
            spectra[1, :, :, :half_width] + spectra[0, :, :, half_width:],
        ]
    )
    return inverse_rows(joined)


def shards(signal, grad_out, filter_taps, skip_gain):
    channels = filter_taps.shape[1]
    signal_rows = signal[0].astype(jnp.float32)
    grad_rows = grad_out[0].astype(jnp.float32)
    tap_half = filter_taps.shape[1] // 2
    columns = jnp.concatenate(
        [signal_rows, filter_taps[:, :tap_half], grad_rows, filter_taps[:, tap_half:]], axis=1
    )
    first, second = split_pairs(forward_spectra(columns))
    signal_spec = first[:, :, :, :channels]
    grad_spec = second[:, :, :, :channels]
    own_spec = jnp.concatenate([first[:, :, :, channels:], second[:, :, :, channels:]], axis=3)
    input_spec = jnp.stack(
        [
            grad_spec[0] * own_spec[0] + grad_spec[1] * own_spec[1],
            grad_spec[1] * own_spec[0] - grad_spec[0] * own_spec[1],
        ]
    )
    filter_terms = jnp.stack(
        [
            grad_spec[0] * signal_spec[0] + grad_spec[1] * signal_spec[1],
            grad_spec[1] * signal_spec[0] - grad_spec[0] * signal_spec[1],
        ]
    )
    summed = lax.psum(filter_terms, "batch")
    rows_back = invert_all(jnp.concatenate([input_spec, summed], axis=3))
    filter_grad = rows_back[:, channels:]
    input_grad = (rows_back[:, :channels] + skip_gain[None, :] * grad_rows).astype(jnp.bfloat16)
    return (input_grad[None], filter_grad)


def solution(mesh):
    groups, seqs = mesh.shape["batch"], mesh.shape["seq"]

    def either(signal, grad_out, filter_taps, skip_gain):
        if fits_fused(groups, seqs, signal, filter_taps):
            return fused_shards(groups, seqs, signal, grad_out, filter_taps, skip_gain)
        return shards(signal, grad_out, filter_taps, skip_gain)

    return jax.shard_map(
        either,
        mesh=mesh,
        in_specs=(P("batch", "seq", None), P("batch", "seq", None), P("seq", None), P()),
        out_specs=(P("batch", "seq", None), P("seq", None)),
        check_vma=False,
    )
```

profile of v0, /device:TPU:0, one launch (start us, length us, event | category | flops | bytes accessed | tf_op | source)
XLA Modules:
  0.0 35.4 jit_solution(4444588975300956239)
XLA Ops:
  0.6 32.4 %shard_map.95 = (bf16[256,256]{1,0:T(8,128)(2,1)}, f32[256,256]{1,0:T(8,128)}) custom-call(bf16[256,256]{1,0:T(8,128)(2,1)} %bitcast.4, bf16[256,256]{1,0:T(8,128)(2,1)} %bitcast.5, f32[256,256]{1,0:T(8,128)} %tap_hbm.1, f32[1,256]{1,0:T(1,128)} %bitcast.7, bf16[512,512]{1,0:T(8,128)(2,1)} %constant.8.clone.high_hbm, ...), custom_call_target="tpu_custom_call" | custom-call | tf_op jit(solution)/shard_map/pallas_call | solution.py:380
  33.1 0.0 copy-start
  33.1 1.6 %copy.12 = bf16[1,256,256]{2,1,0:T(8,128)(2,1)} copy(bf16[1,256,256]{2,1,0:T(8,128)(2,1)} %bitcast.6) | data formatting | bytes 262144
  34.7 0.0 copy-done
  34.7 0.7 %copy.13 = f32[256,256]{1,0:T(8,128)} copy(f32[256,256]{1,0:T(8,128)S(1)} %copy-done) | data formatting | bytes 524288
Async XLA Ops:
  33.1 1.6 %copy-start = (f32[256,256]{1,0:T(8,128)S(1)}, f32[256,256]{1,0:T(8,128)}, u32[]{:S(2)}) copy-start(f32[256,256]{1,0:T(8,128)} %get-tuple-element.9) | copy-start | bytes 786436
where the time goes:
time: 36 us; the launch traced here: 35.4 us
  Pallas kernels  32.4 us (90%)
  local copies, waits for them, and re-layouts  2.32 us (6%)
  between operations  0.65 us (2%)
    pallas_call x1, Pallas kernels, fused_shards(): pl.pallas_call(functools.partial(fused_kernel, groups, seqs), out_shape=(...  32.4 us
    unnamed x4, local copies, waits for them, and re-layouts  2.32 us

commit v1 on v0

--- a/solution.py
+++ b/solution.py
@@ -93,12 +93,12 @@
 def fused_kernel(
     groups, seqs,
     signal_hbm, grad_hbm, tap_hbm, skip_hbm, high_hbm, low_hbm, cos_hbm, sin_hbm,
-    input_hbm, filter_hbm,
+    input_in, filter_in, skip_term_ref,
     signal_ref, grad_ref, tap_ref, skip_ref, high_ref, low_ref, cos_ref, sin_ref,
     grad_out_buf, signal_out_buf, tap_out_buf, grad_in, signal_in, tap_in,
-    input_out, filter_out, input_in, filter_in,
+    input_out, filter_out,
     tap_rows, tap_spec, grad_rows, grad_spec, signal_rows, signal_spec, input_rows, filter_rows, filter_spec,
-    input_ref, filter_ref, send_sems, recv_sems, load_sems,
+    send_sems, recv_sems, load_sems,
 ):
     count = groups * seqs
     coarse = seqs + 1
@@ -322,32 +322,40 @@
     filter_in[parity, pair * seqs + seq] = filter_out[seq]
 
     half = count // 2
+    skip_term_ref[...] = skip_ref[...] * grad_ref[...].astype(F32)
     all_of(input_in, count - 1, INPUT).wait_recv()
-    gradient = input_in[...].reshape(channels, rows).T + skip_ref[...] * grad_ref[...].astype(F32)
-    input_ref[...] = gradient.astype(BF16)
-    input_store = load(len(loads), input_ref, input_hbm)
-    input_store.start()
     all_of(filter_in.at[0], half - 1, FILTER).wait_recv()
     mine = filter_in.at[parity]
     partner = 2 * pair + 1 - parity
     forward = transfer(mine, mine, FORWARD, partner, seq)
     forward.start()
     forward.wait_recv()
-    parts = [
-        filter_in[which, first * seqs : (first + 1) * seqs].reshape(seqs * own, rows)
-        for first in range(half_groups)
-        for which in range(2)
-    ]
-    filter_ref[...] = jnp.concatenate(parts, axis=0).T
-    filter_store = load(len(loads) + 1, filter_ref, filter_hbm)
-    filter_store.start()
     for kind, buffer in ((GRAD, grad_in), (SIGNAL, signal_in), (INPUT, input_in)):
         all_of(buffer, count - 1, kind).wait_send()
     all_of(filter_in.at[0], half - 1, FILTER).wait_send()
     forward.wait_send()
+    all_of(tap_in, seqs - 1, TAPS).wait_send()
+
+
+def finish_kernel(
+    groups, seqs, input_in, filter_in, skip_term_ref, input_hbm, filter_hbm, input_ref, filter_ref, sems
+):
+    own, rows = input_in.shape[1:]
+    channels = input_in.shape[0] * own
+    gradient = input_in[...].reshape(channels, rows).T + skip_term_ref[...]
+    input_ref[...] = gradient.astype(BF16)
+    input_store = pltpu.make_async_copy(input_ref, input_hbm, sems.at[0])
+    input_store.start()
+    parts = [
+        filter_in[which, first * seqs : (first + 1) * seqs].reshape(seqs * own, rows)
+        for first in range(groups // 2)
+        for which in range(2)
+    ]
+    filter_ref[...] = jnp.concatenate(parts, axis=0).T
+    filter_store = pltpu.make_async_copy(filter_ref, filter_hbm, sems.at[1])
+    filter_store.start()
     input_store.wait()
     filter_store.wait()
-    all_of(tap_in, seqs - 1, TAPS).wait_send()
 
 
 def fine_tables(rows):
@@ -377,34 +385,54 @@
     hbm = pl.BlockSpec(memory_space=pltpu.HBM)
     turns = pltpu.VMEM((coarse, own, rows), F32)
     table = pltpu.VMEM((2 * rows, 2 * rows), BF16)
-    input_grad, filter_grad = pl.pallas_call(
+    vmem = pl.BlockSpec(memory_space=pltpu.VMEM)
+    gathered = pl.pallas_call(
         functools.partial(fused_kernel, groups, seqs),
         out_shape=(
-            jax.ShapeDtypeStruct((rows, channels), BF16),
-            jax.ShapeDtypeStruct((rows, channels), F32),
+            pltpu.VMEM((count, own, rows), F32),
+            pltpu.VMEM((2, count // 2, own, rows), F32),
+            pltpu.VMEM((rows, channels), F32),
         ),
         in_specs=[hbm] * 8,
-        out_specs=(hbm, hbm),
+        out_specs=(vmem, vmem, vmem),
         scratch_shapes=[
             pltpu.VMEM((rows, channels), BF16), pltpu.VMEM((rows, channels), BF16),
             pltpu.VMEM((rows, channels), F32), pltpu.VMEM((1, channels), F32),
             table, table, turns, turns,
             blocks, blocks, blocks, blocks, blocks, few,
-            blocks, few, blocks, pltpu.VMEM((2, count // 2, own, rows), F32),
+            blocks, few,
             lines(1), lines(1), pairs, pairs, lines(groups), lines(groups),
             pairs, lines(1), lines(1),
-            pltpu.VMEM((rows, channels), BF16), pltpu.VMEM((rows, channels), F32),
             pltpu.SemaphoreType.DMA((6,)),
             pltpu.SemaphoreType.DMA((6,)),
-            pltpu.SemaphoreType.DMA((10,)),
+            pltpu.SemaphoreType.DMA((8,)),
         ],
         compiler_params=pltpu.CompilerParams(
-            collective_id=0, has_side_effects=True, vmem_limit_bytes=67_043_328
+            collective_id=0, has_side_effects=True, vmem_limit_bytes=24 << 20
         ),
     )(
-        signal[0], grad_out[0], filter_taps, skip_gain[None, :],
-        jnp.asarray(high), jnp.asarray(low), jnp.asarray(cos_turn), jnp.asarray(sin_turn),
-    )
+        *(
+            pltpu.with_memory_space_constraint(array, pltpu.HBM)
+            for array in (
+                signal[0], grad_out[0], filter_taps, skip_gain[None, :],
+                jnp.asarray(high), jnp.asarray(low), jnp.asarray(cos_turn), jnp.asarray(sin_turn),
+            )
+        )
+    )
+    input_grad, filter_grad = pl.pallas_call(
+        functools.partial(finish_kernel, groups, seqs),
+        out_shape=(
+            jax.ShapeDtypeStruct((rows, channels), BF16),
+            jax.ShapeDtypeStruct((rows, channels), F32),
+        ),
+        in_specs=[vmem] * 3,
+        out_specs=(hbm, hbm),
+        scratch_shapes=[
+            pltpu.VMEM((rows, channels), BF16), pltpu.VMEM((rows, channels), F32),
+            pltpu.SemaphoreType.DMA((2,)),
+        ],
+        compiler_params=pltpu.CompilerParams(vmem_limit_bytes=24 << 20),
+    )(*gathered)
     return input_grad[None], filter_grad
 
 

time: 36 us -> 33.8 us (0.939); the launches traced: 35.4 us -> 33.7 us
  local copies, waits for them, and re-layouts: 2.32 us -> 0 us
  Pallas kernels: 32.4 us -> 33.1 us
    unnamed x4 -> x0, local copies, waits for them, and re-layouts: 2.32 us -> none
    pallas_call x0 -> x1, Pallas kernels: none -> 0.92 us  [fused_shards(): pl.pallas_call(functools.partial(finish_kernel, groups, seqs), out_shape=...]
where the time goes in v1:
time: 33.8 us; the launch traced here: 33.7 us
  Pallas kernels  33.1 us (98%)
  between operations  0.64 us (2%)
    pallas_call x1, Pallas kernels, fused_shards(): pl.pallas_call(functools.partial(fused_kernel, groups, seqs), out_shape=(...  32.1 us
    pallas_call x1, Pallas kernels, fused_shards(): pl.pallas_call(functools.partial(finish_kernel, groups, seqs), out_shape=...  0.92 us

profile of v1, /device:TPU:0, one launch (start us, length us, event | category | flops | bytes accessed | tf_op | source)
XLA Modules:
  0.0 33.7 jit_solution(8405193056764469507)
XLA Ops:
  0.6 32.1 %shard_map.95 = (f32[32,8,256]{2,1,0:T(8,128)S(1)}, f32[2,16,8,256]{3,2,1,0:T(8,128)S(1)}, f32[256,256]{1,0:T(8,128)S(1)}) custom-call(bf16[256,256]{1,0:T(8,128)(2,1)} %bitcast.4, bf16[256,256]{1,0:T(8,128)(2,1)} %bitcast.5, f32[256,256]{1,0:T(8,128)} %tap_hbm.1, f32[1,256]{1,0:T(1,128)} %bitcast.6, bf16[512,512]{1,0:T(8,128)(2,1)} %constant.8.clone.high_hbm, ...), custom_call_target="tpu_custom_call" | custom-call | tf_op jit(solution)/shard_map/pallas_call | solution.py:389
  32.8 0.9 %shard_map.96 = (bf16[256,256]{1,0:T(8,128)(2,1)}, f32[256,256]{1,0:T(8,128)}) custom-call(f32[32,8,256]{2,1,0:T(8,128)S(1)} %get-tuple-element.7.input_in, f32[2,16,8,256]{3,2,1,0:T(8,128)S(1)} %get-tuple-element.8.filter_in, f32[256,256]{1,0:T(8,128)S(1)} %get-tuple-element.9.skip_term_ref), custom_call_target="tpu_custom_call" | custom-call | tf_op jit(solution)/shard_map/pallas_call | solution.py:422

commit v2 on v1

--- a/solution.py
+++ b/solution.py
@@ -98,7 +98,7 @@
     grad_out_buf, signal_out_buf, tap_out_buf, grad_in, signal_in, tap_in,
     input_out, filter_out,
     tap_rows, tap_spec, grad_rows, grad_spec, signal_rows, signal_spec, input_rows, filter_rows, filter_spec,
-    send_sems, recv_sems, load_sems,
+    send_sems, recv_sems, load_sems, ready_sems,
 ):
     count = groups * seqs
     coarse = seqs + 1
@@ -111,7 +111,7 @@
 
     parity, pair = lax.rem(group, 2), lax.div(group, 2)
     half_seqs, half_groups = seqs // 2, groups // 2
-    upper, inner = lax.div(seq, half_seqs), lax.rem(seq, half_seqs)
+    rank = seq * groups + group
 
     def load(index, source, target):
         return pltpu.make_async_copy(source, target, load_sems.at[index])
@@ -130,28 +130,30 @@
     loads[TAPS].start()
 
     def seq_at(step):
-        other = lax.rem(upper + 1 + lax.div(step, half_seqs), 2)
-        return other * half_seqs + lax.rem(inner + step, half_seqs)
-
-    def peer(step):
-        to_seq = seq_at(lax.div(step, groups))
-        to_group = lax.rem(group + step, groups)
-        return to_group * seqs + to_seq, to_group, to_seq
-
-    def over_peers(body, total, own_step):
-        lax.fori_loop(0, own_step, body, 0, unroll=min(4, own_step))
-        lax.fori_loop(own_step + 1, total, body, 0, unroll=min(3, total - own_step - 1))
+        return lax.bitwise_xor(seq, lax.rem(step + half_seqs, seqs))
+
+    def over_seqs(body):
+        lax.fori_loop(0, half_seqs, body, 0)
+        lax.fori_loop(half_seqs + 1, seqs, body, 0)
+
+    def groups_of(to_seq):
+        for flip in range(groups):
+            to_group = lax.bitwise_xor(group, flip)
+            yield flip, to_group, to_seq * groups + to_group
+
+    def signal(semaphore, to_group, to_seq):
+        pl.semaphore_signal(
+            semaphore, inc=1, device_id={"batch": to_group, "seq": to_seq}, device_id_type=MESH
+        )
 
     barrier = pltpu.get_barrier_semaphore()
 
     def greet(step, carry):
-        _, to_group, to_seq = peer(step)
-        pl.semaphore_signal(
-            barrier, inc=1, device_id={"batch": to_group, "seq": to_seq}, device_id_type=MESH
-        )
+        for _, to_group, to_rank in groups_of(seq_at(step)):
+            pl.when(to_rank > rank)(lambda: signal(barrier, to_group, seq_at(step)))
         return carry
 
-    over_peers(greet, count, half_seqs * groups)
+    lax.fori_loop(0, seqs, greet, 0)
     for copy in loads[2:]:
         copy.start()
 
@@ -166,37 +168,66 @@
         )
 
     def all_of(buffer, blocks, kind):
-        _, to_group, to_seq = peer(0)
         view = buffer.at[pl.ds(0, blocks)]
-        return transfer(view, view, kind, to_group, to_seq)
+        return transfer(view, view, kind, group, seq_at(0))
 
     loads[GRAD].wait()
     grad_out_buf[...] = grad_ref[...].astype(F32).T.reshape(count, own, rows)
     loads[TAPS].wait()
     tap_out_buf[...] = tap_ref[...].T.reshape(count, own, rows)
-    pl.semaphore_wait(barrier, count - 1)
-
-    def send_taps(step, carry):
+    pl.when(rank > 0)(lambda: pl.semaphore_wait(barrier, rank))
+
+    def answer(step, carry):
+        for _, to_group, to_rank in groups_of(seq_at(step)):
+            pl.when(to_rank < rank)(lambda: signal(ready_sems.at[seq], to_group, seq_at(step)))
+        return carry
+
+    lax.fori_loop(0, seqs, answer, 0)
+
+    def send_first(flip, to_group, to_seq):
+        place = to_group * seqs + to_seq
+        if flip == 0:
+            transfer(tap_out_buf.at[place], tap_in.at[seq], TAPS, to_group, to_seq).start()
+        transfer(grad_out_buf.at[place], grad_in.at[me], GRAD, to_group, to_seq).start()
+
+    def send_lower(step, carry):
         to_seq = seq_at(step)
-        place = group * seqs + to_seq
-        transfer(tap_out_buf.at[place], tap_in.at[seq], TAPS, group, to_seq).start()
+        for flip, to_group, to_rank in groups_of(to_seq):
+            pl.when(to_rank < rank)(lambda: send_first(flip, to_group, to_seq))
         return carry
 
-    def send_grads(step, carry):
-        place, to_group, to_seq = peer(step)
-        transfer(grad_out_buf.at[place], grad_in.at[me], GRAD, to_group, to_seq).start()
+    def send_higher(step, carry):
+        to_seq = lax.bitwise_xor(step, lax.rem(seq, 2))
+
+        @pl.when((to_seq == seq) & (group < groups - 1))
+        def _():
+            pl.semaphore_wait(ready_sems.at[seq], groups - 1 - group)
+
+        @pl.when(to_seq > seq)
+        def _():
+            pl.semaphore_wait(ready_sems.at[to_seq], groups)
+
+        for flip, to_group, to_rank in groups_of(to_seq):
+            pl.when(to_rank > rank)(lambda: send_first(flip, to_group, to_seq))
         return carry
 
-    def send_signals(step, carry):
-        place, to_group, to_seq = peer(step)
-        transfer(signal_out_buf.at[place], signal_in.at[me], SIGNAL, to_group, to_seq).start()
-        return carry
-
-    over_peers(send_taps, seqs, half_seqs)
-    over_peers(send_grads, count, half_seqs * groups)
+    lax.fori_loop(0, seqs, send_lower, 0)
+    lax.fori_loop(0, seqs, send_higher, 0)
     loads[SIGNAL].wait()
     signal_out_buf[...] = signal_ref[...].astype(F32).T.reshape(count, own, rows)
-    over_peers(send_signals, count, half_seqs * groups)
+
+    def send_signal(to_group, to_seq):
+        place = to_group * seqs + to_seq
+        transfer(signal_out_buf.at[place], signal_in.at[me], SIGNAL, to_group, to_seq).start()
+
+    def send_signals(step, carry):
+        for _, to_group, _ in groups_of(seq_at(step)):
+            send_signal(to_group, seq_at(step))
+        return carry
+
+    over_seqs(send_signals)
+    for flip in range(1, groups):
+        send_signal(lax.bitwise_xor(group, flip), seq)
     grad_in[me] = grad_out_buf[me]
     tap_in[seq] = tap_out_buf[me]
     signal_in[me] = signal_out_buf[me]
@@ -269,17 +300,22 @@
 
         lax.fori_loop(0, 2, collect_input, 0)
 
-        def send_inputs(step, carry):
-            to_seq = seq_at(lax.div(step, 2))
-            to_group = group_at(2 * first + lax.rem(parity + step, 2))
-            place = to_group * seqs + to_seq
-            transfer(input_out.at[place], input_in.at[me], INPUT, to_group, to_seq).start()
-            return carry
-
         if first == 0:
-            over_peers(send_inputs, 2 * seqs, 2 * half_seqs)
+            partner = lax.bitwise_xor(group, 1)
+            lax.fori_loop(0, seqs, lambda step, carry: send_input(partner, seq_at(step)), 0)
         else:
-            lax.fori_loop(0, 2 * seqs, send_inputs, 0)
+
+            def send_inputs(step, carry):
+                for index in range(2):
+                    send_input(group_at(2 * first + lax.bitwise_xor(parity, index)), seq_at(step))
+                return carry
+
+            lax.fori_loop(0, seqs, send_inputs, 0)
+
+    def send_input(to_group, to_seq):
+        place = to_group * seqs + to_seq
+        transfer(input_out.at[place], input_in.at[me], INPUT, to_group, to_seq).start()
+        return 0
 
     for first in reversed(range(half_groups)):
         input_part(first)
@@ -309,16 +345,22 @@
     for s, block in enumerate(collect(filter_spec, 0)):
         filter_out[s] = block
 
-    def send_filters(step, carry):
-        to_seq = seq_at(lax.div(step, half_groups))
-        to_group = 2 * lax.rem(pair + step, half_groups) + parity
+    def send_filter(turned, to_seq):
+        to_group = 2 * lax.rem(pair + turned, half_groups) + parity
         place = pair * seqs + seq
         transfer(
             filter_out.at[to_seq], filter_in.at[parity, place], FILTER, to_group, to_seq
         ).start()
+
+    def send_filters(step, carry):
+        for turned in range(half_groups):
+            send_filter(turned, seq_at(step))
         return carry
 
-    over_peers(send_filters, seqs * half_groups, half_seqs * half_groups)
+    over_seqs(send_filters)
+    for turned in range(1, half_groups):
+        send_filter(turned, seq)
+    over_seqs(lambda step, carry: send_input(group, seq_at(step)))
     filter_in[parity, pair * seqs + seq] = filter_out[seq]
 
     half = count // 2
@@ -406,6 +448,7 @@
             pltpu.SemaphoreType.DMA((6,)),
             pltpu.SemaphoreType.DMA((6,)),
             pltpu.SemaphoreType.DMA((8,)),
+            pltpu.SemaphoreType.REGULAR((seqs,)),
         ],
         compiler_params=pltpu.CompilerParams(
             collective_id=0, has_side_effects=True, vmem_limit_bytes=24 << 20
@@ -444,6 +487,8 @@
         and groups % 2 == 0
         and rows % 128 == 0
         and channels % (8 * groups * seqs) == 0
+        and groups & (groups - 1) == 0
+        and seqs & (seqs - 1) == 0
     )
 
 

time: 33.8 us -> 36.3 us (1.074)
  Pallas kernels: 33.1 us -> 35.5 us
    pallas_call x1, Pallas kernels: 32.1 us -> 34.6 us  [fused_shards(): pl.pallas_call(functools.partial(fused_kernel, groups, seqs), out_shape=(...]
where the time goes in v2:
time: 36.3 us; the launch traced here: 36.1 us
  Pallas kernels  35.5 us (98%)
  between operations  0.64 us (2%)
    pallas_call x1, Pallas kernels, fused_shards(): pl.pallas_call(functools.partial(fused_kernel, groups, seqs), out_shape=(...  34.6 us
    pallas_call x1, Pallas kernels, fused_shards(): pl.pallas_call(functools.partial(finish_kernel, groups, seqs), out_shape=...  0.92 us

profile of v2, /device:TPU:0, one launch (start us, length us, event | category | flops | bytes accessed | tf_op | source)
XLA Modules:
  0.0 36.1 jit_solution(9830680519549878848)
XLA Ops:
  0.6 34.6 %shard_map.95 = (f32[32,8,256]{2,1,0:T(8,128)S(1)}, f32[2,16,8,256]{3,2,1,0:T(8,128)S(1)}, f32[256,256]{1,0:T(8,128)S(1)}) custom-call(bf16[256,256]{1,0:T(8,128)(2,1)} %bitcast.4, bf16[256,256]{1,0:T(8,128)(2,1)} %bitcast.5, f32[256,256]{1,0:T(8,128)} %tap_hbm.1, f32[1,256]{1,0:T(1,128)} %bitcast.6, bf16[512,512]{1,0:T(8,128)(2,1)} %constant.8.clone.high_hbm, ...), custom_call_target="tpu_custom_call" | custom-call | tf_op jit(solution)/shard_map/pallas_call | solution.py:431
  35.2 0.9 %shard_map.96 = (bf16[256,256]{1,0:T(8,128)(2,1)}, f32[256,256]{1,0:T(8,128)}) custom-call(f32[32,8,256]{2,1,0:T(8,128)S(1)} %get-tuple-element.7.input_in, f32[2,16,8,256]{3,2,1,0:T(8,128)S(1)} %get-tuple-element.8.filter_in, f32[256,256]{1,0:T(8,128)S(1)} %get-tuple-element.9.skip_term_ref), custom_call_target="tpu_custom_call" | custom-call | tf_op jit(solution)/shard_map/pallas_call | solution.py:465

commit v3 on v1

--- a/solution.py
+++ b/solution.py
@@ -93,10 +93,10 @@
 def fused_kernel(
     groups, seqs,
     signal_hbm, grad_hbm, tap_hbm, skip_hbm, high_hbm, low_hbm, cos_hbm, sin_hbm,
-    input_in, filter_in, skip_term_ref,
+    input_ref, filter_in,
     signal_ref, grad_ref, tap_ref, skip_ref, high_ref, low_ref, cos_ref, sin_ref,
     grad_out_buf, signal_out_buf, tap_out_buf, grad_in, signal_in, tap_in,
-    input_out, filter_out,
+    input_out, filter_out, input_in,
     tap_rows, tap_spec, grad_rows, grad_spec, signal_rows, signal_spec, input_rows, filter_rows, filter_spec,
     send_sems, recv_sems, load_sems,
 ):
@@ -129,29 +129,33 @@
     loads[GRAD].start()
     loads[TAPS].start()
 
-    def seq_at(step):
-        other = lax.rem(upper + 1 + lax.div(step, half_seqs), 2)
-        return other * half_seqs + lax.rem(inner + step, half_seqs)
-
-    def peer(step):
-        to_seq = seq_at(lax.div(step, groups))
-        to_group = lax.rem(group + step, groups)
-        return to_group * seqs + to_seq, to_group, to_seq
-
-    def over_peers(body, total, own_step):
-        lax.fori_loop(0, own_step, body, 0, unroll=min(4, own_step))
-        lax.fori_loop(own_step + 1, total, body, 0, unroll=min(3, total - own_step - 1))
+    rank = seq * groups + group
+    turns = [(half_seqs + seqs - step) % seqs for step in range(seqs)]
+
+    def turned_seq(offset):
+        return lax.rem(seq + offset, seqs) if offset else seq
+
+    def over_peers(body):
+        for shift in (half_groups, *range(half_groups - 1, -1, -1), *range(half_groups + 1, groups)):
+            to_group = lax.rem(group + shift, groups) if shift else group
+            for offset in reversed(range(seqs)):
+                if shift or offset:
+                    body(to_group, turned_seq(offset), shift == 0)
+
+    def compare(to_group, to_seq):
+        return to_seq * groups + to_group - rank
+
+    def signal(semaphore, to_group, to_seq):
+        pl.semaphore_signal(
+            semaphore, inc=1, device_id={"batch": to_group, "seq": to_seq}, device_id_type=MESH
+        )
 
     barrier = pltpu.get_barrier_semaphore()
 
-    def greet(step, carry):
-        _, to_group, to_seq = peer(step)
-        pl.semaphore_signal(
-            barrier, inc=1, device_id={"batch": to_group, "seq": to_seq}, device_id_type=MESH
-        )
-        return carry
-
-    over_peers(greet, count, half_seqs * groups)
+    def greet(to_group, to_seq, same):
+        signal(barrier, to_group, to_seq)
+
+    over_peers(greet)
     for copy in loads[2:]:
         copy.start()
 
@@ -166,37 +170,29 @@
         )
 
     def all_of(buffer, blocks, kind):
-        _, to_group, to_seq = peer(0)
         view = buffer.at[pl.ds(0, blocks)]
-        return transfer(view, view, kind, to_group, to_seq)
+        return transfer(view, view, kind, group, turned_seq(1))
 
     loads[GRAD].wait()
     grad_out_buf[...] = grad_ref[...].astype(F32).T.reshape(count, own, rows)
     loads[TAPS].wait()
     tap_out_buf[...] = tap_ref[...].T.reshape(count, own, rows)
+
+    def send_grad(to_group, to_seq, same):
+        place = to_group * seqs + to_seq
+        if same:
+            transfer(tap_out_buf.at[place], tap_in.at[seq], TAPS, to_group, to_seq).start()
+        transfer(grad_out_buf.at[place], grad_in.at[me], GRAD, to_group, to_seq).start()
+
+    def send_signal(to_group, to_seq, same):
+        place = to_group * seqs + to_seq
+        transfer(signal_out_buf.at[place], signal_in.at[me], SIGNAL, to_group, to_seq).start()
+
     pl.semaphore_wait(barrier, count - 1)
-
-    def send_taps(step, carry):
-        to_seq = seq_at(step)
-        place = group * seqs + to_seq
-        transfer(tap_out_buf.at[place], tap_in.at[seq], TAPS, group, to_seq).start()
-        return carry
-
-    def send_grads(step, carry):
-        place, to_group, to_seq = peer(step)
-        transfer(grad_out_buf.at[place], grad_in.at[me], GRAD, to_group, to_seq).start()
-        return carry
-
-    def send_signals(step, carry):
-        place, to_group, to_seq = peer(step)
-        transfer(signal_out_buf.at[place], signal_in.at[me], SIGNAL, to_group, to_seq).start()
-        return carry
-
-    over_peers(send_taps, seqs, half_seqs)
-    over_peers(send_grads, count, half_seqs * groups)
+    over_peers(send_grad)
     loads[SIGNAL].wait()
     signal_out_buf[...] = signal_ref[...].astype(F32).T.reshape(count, own, rows)
-    over_peers(send_signals, count, half_seqs * groups)
+    over_peers(send_signal)
     grad_in[me] = grad_out_buf[me]
     tap_in[seq] = tap_out_buf[me]
     signal_in[me] = signal_out_buf[me]
@@ -269,17 +265,13 @@
 
         lax.fori_loop(0, 2, collect_input, 0)
 
-        def send_inputs(step, carry):
-            to_seq = seq_at(lax.div(step, 2))
-            to_group = group_at(2 * first + lax.rem(parity + step, 2))
-            place = to_group * seqs + to_seq
-            transfer(input_out.at[place], input_in.at[me], INPUT, to_group, to_seq).start()
-            return carry
-
-        if first == 0:
-            over_peers(send_inputs, 2 * seqs, 2 * half_seqs)
-        else:
-            lax.fori_loop(0, 2 * seqs, send_inputs, 0)
+        for offset in turns:
+            for flip in range(2):
+                if first or offset or flip:
+                    to_group = group_at(2 * first + lax.rem(parity + flip, 2))
+                    to_seq = turned_seq(offset)
+                    place = to_group * seqs + to_seq
+                    transfer(input_out.at[place], input_in.at[me], INPUT, to_group, to_seq).start()
 
     for first in reversed(range(half_groups)):
         input_part(first)
@@ -309,21 +301,20 @@
     for s, block in enumerate(collect(filter_spec, 0)):
         filter_out[s] = block
 
-    def send_filters(step, carry):
-        to_seq = seq_at(lax.div(step, half_groups))
-        to_group = 2 * lax.rem(pair + step, half_groups) + parity
-        place = pair * seqs + seq
-        transfer(
-            filter_out.at[to_seq], filter_in.at[parity, place], FILTER, to_group, to_seq
-        ).start()
-        return carry
-
-    over_peers(send_filters, seqs * half_groups, half_seqs * half_groups)
+    for offset in turns:
+        for flip in range(half_groups):
+            if offset or flip:
+                to_group = 2 * lax.rem(pair + flip, half_groups) + parity
+                to_seq = turned_seq(offset)
+                transfer(
+                    filter_out.at[to_seq], filter_in.at[parity, pair * seqs + seq], FILTER, to_group, to_seq
+                ).start()
     filter_in[parity, pair * seqs + seq] = filter_out[seq]
 
     half = count // 2
-    skip_term_ref[...] = skip_ref[...] * grad_ref[...].astype(F32)
     all_of(input_in, count - 1, INPUT).wait_recv()
+    gradient = input_in[...].reshape(channels, rows).T + skip_ref[...] * grad_ref[...].astype(F32)
+    input_ref[...] = gradient.astype(BF16)
     all_of(filter_in.at[0], half - 1, FILTER).wait_recv()
     mine = filter_in.at[parity]
     partner = 2 * pair + 1 - parity
@@ -337,13 +328,8 @@
     all_of(tap_in, seqs - 1, TAPS).wait_send()
 
 
-def finish_kernel(
-    groups, seqs, input_in, filter_in, skip_term_ref, input_hbm, filter_hbm, input_ref, filter_ref, sems
-):
-    own, rows = input_in.shape[1:]
-    channels = input_in.shape[0] * own
-    gradient = input_in[...].reshape(channels, rows).T + skip_term_ref[...]
-    input_ref[...] = gradient.astype(BF16)
+def finish_kernel(groups, seqs, input_ref, filter_in, input_hbm, filter_hbm, filter_ref, sems):
+    own, rows = filter_in.shape[2:]
     input_store = pltpu.make_async_copy(input_ref, input_hbm, sems.at[0])
     input_store.start()
     parts = [
@@ -389,18 +375,17 @@
     gathered = pl.pallas_call(
         functools.partial(fused_kernel, groups, seqs),
         out_shape=(
-            pltpu.VMEM((count, own, rows), F32),
+            pltpu.VMEM((rows, channels), BF16),
             pltpu.VMEM((2, count // 2, own, rows), F32),
-            pltpu.VMEM((rows, channels), F32),
         ),
         in_specs=[hbm] * 8,
-        out_specs=(vmem, vmem, vmem),
+        out_specs=(vmem, vmem),
         scratch_shapes=[
             pltpu.VMEM((rows, channels), BF16), pltpu.VMEM((rows, channels), BF16),
             pltpu.VMEM((rows, channels), F32), pltpu.VMEM((1, channels), F32),
             table, table, turns, turns,
             blocks, blocks, blocks, blocks, blocks, few,
-            blocks, few,
+            blocks, few, blocks,
             lines(1), lines(1), pairs, pairs, lines(groups), lines(groups),
             pairs, lines(1), lines(1),
             pltpu.SemaphoreType.DMA((6,)),
@@ -425,10 +410,10 @@
             jax.ShapeDtypeStruct((rows, channels), BF16),
             jax.ShapeDtypeStruct((rows, channels), F32),
         ),
-        in_specs=[vmem] * 3,
+        in_specs=[vmem] * 2,
         out_specs=(hbm, hbm),
         scratch_shapes=[
-            pltpu.VMEM((rows, channels), BF16), pltpu.VMEM((rows, channels), F32),
+            pltpu.VMEM((rows, channels), F32),
             pltpu.SemaphoreType.DMA((2,)),
         ],
         compiler_params=pltpu.CompilerParams(vmem_limit_bytes=24 << 20),

time: 33.8 us -> 31.9 us (0.944)
  Pallas kernels: 33.1 us -> 31.1 us
    pallas_call x1, Pallas kernels: 32.1 us -> 30.3 us  [fused_shards(): pl.pallas_call(functools.partial(fused_kernel, groups, seqs), out_shape=(...]
where the time goes in v3:
time: 31.9 us; the launch traced here: 31.8 us
  Pallas kernels  31.1 us (97%)
  between operations  0.64 us (2%)
    pallas_call x1, Pallas kernels, fused_shards(): pl.pallas_call(functools.partial(fused_kernel, groups, seqs), out_shape=(...  30.3 us
    pallas_call x1, Pallas kernels, fused_shards(): pl.pallas_call(functools.partial(finish_kernel, groups, seqs), out_shape=...  0.86 us

profile of v3, /device:TPU:0, one launch (start us, length us, event | category | flops | bytes accessed | tf_op | source)
XLA Modules:
  0.0 31.8 jit_solution(15864716701362027597)
XLA Ops:
  0.6 30.3 %shard_map.95 = (bf16[256,256]{1,0:T(8,128)(2,1)S(1)}, f32[2,16,8,256]{3,2,1,0:T(8,128)S(1)}) custom-call(bf16[256,256]{1,0:T(8,128)(2,1)} %bitcast.4, bf16[256,256]{1,0:T(8,128)(2,1)} %bitcast.5, f32[256,256]{1,0:T(8,128)} %tap_hbm.1, f32[1,256]{1,0:T(1,128)} %bitcast.6, bf16[512,512]{1,0:T(8,128)(2,1)} %constant.8.clone.high_hbm, ...), custom_call_target="tpu_custom_call" | custom-call | tf_op jit(solution)/shard_map/pallas_call | solution.py:375
  30.9 0.9 %shard_map.96 = (bf16[256,256]{1,0:T(8,128)(2,1)}, f32[256,256]{1,0:T(8,128)}) custom-call(bf16[256,256]{1,0:T(8,128)(2,1)S(1)} %get-tuple-element.6.input_ref, f32[2,16,8,256]{3,2,1,0:T(8,128)S(1)} %get-tuple-element.7.filter_in), custom_call_target="tpu_custom_call" | custom-call | tf_op jit(solution)/shard_map/pallas_call | solution.py:407

commit v4 on v3

--- a/solution.py
+++ b/solution.py
@@ -12,7 +12,7 @@
 MESH = pl.DeviceIdType.MESH
 F32 = jnp.float32
 BF16 = jnp.bfloat16
-GRAD, TAPS, SIGNAL, INPUT, FILTER, FORWARD = range(6)
+GRAD, TAPS, SIGNAL, INPUT, FILTER, FORWARD, CROSS, NEAR_GRAD, NEAR_SIGNAL, NEAR_TAPS, PART, NEAR_INPUT = range(12)
 
 
 def weighted(terms):
@@ -98,6 +98,8 @@
     grad_out_buf, signal_out_buf, tap_out_buf, grad_in, signal_in, tap_in,
     input_out, filter_out, input_in,
     tap_rows, tap_spec, grad_rows, grad_spec, signal_rows, signal_spec, input_rows, filter_rows, filter_spec,
+    near_grad_in, near_signal_in, near_tap_in, near_input_out, near_input_in, near_filter_out, part_in,
+    near_grad, near_signal, near_tap, near_lines, near_filter,
     send_sems, recv_sems, load_sems,
 ):
     count = groups * seqs
@@ -106,7 +108,6 @@
     channels = count * own
     group, seq = lax.axis_index("batch"), lax.axis_index("seq")
     me = group * seqs + seq
-    scale = 1.0 / (2 * seqs * rows)
     re, im = pl.ds(0, rows), pl.ds(rows, rows)
 
     parity, pair = lax.rem(group, 2), lax.div(group, 2)
@@ -129,21 +130,21 @@
     loads[GRAD].start()
     loads[TAPS].start()
 
-    rank = seq * groups + group
+    slot, near_count = group * half_seqs + inner, groups * half_seqs
+    mate = lax.rem(seq + half_seqs, seqs)
     turns = [(half_seqs + seqs - step) % seqs for step in range(seqs)]
 
     def turned_seq(offset):
         return lax.rem(seq + offset, seqs) if offset else seq
 
+    shifts = (half_groups, *range(half_groups - 1, -1, -1), *range(half_groups + 1, groups))
+
     def over_peers(body):
-        for shift in (half_groups, *range(half_groups - 1, -1, -1), *range(half_groups + 1, groups)):
+        for shift in shifts:
             to_group = lax.rem(group + shift, groups) if shift else group
             for offset in reversed(range(seqs)):
                 if shift or offset:
                     body(to_group, turned_seq(offset), shift == 0)
-
-    def compare(to_group, to_seq):
-        return to_seq * groups + to_group - rank
 
     def signal(semaphore, to_group, to_seq):
         pl.semaphore_signal(
@@ -173,34 +174,98 @@
         view = buffer.at[pl.ds(0, blocks)]
         return transfer(view, view, kind, group, turned_seq(1))
 
+    @pl.when(upper == 0)
+    def _():
+        for where in range(groups):
+            signal_in[where * seqs + half_seqs : (where + 1) * seqs] = jnp.zeros((half_seqs, own, rows), F32)
+
+    @pl.when(upper == 1)
+    def _():
+        for where in range(groups):
+            grad_in[where * seqs : where * seqs + half_seqs] = jnp.zeros((half_seqs, own, rows), F32)
+
     loads[GRAD].wait()
     grad_out_buf[...] = grad_ref[...].astype(F32).T.reshape(count, own, rows)
     loads[TAPS].wait()
     tap_out_buf[...] = tap_ref[...].T.reshape(count, own, rows)
-
-    def send_grad(to_group, to_seq, same):
-        place = to_group * seqs + to_seq
-        if same:
-            transfer(tap_out_buf.at[place], tap_in.at[seq], TAPS, to_group, to_seq).start()
-        transfer(grad_out_buf.at[place], grad_in.at[me], GRAD, to_group, to_seq).start()
-
-    def send_signal(to_group, to_seq, same):
-        place = to_group * seqs + to_seq
-        transfer(signal_out_buf.at[place], signal_in.at[me], SIGNAL, to_group, to_seq).start()
-
-    pl.semaphore_wait(barrier, count - 1)
-    over_peers(send_grad)
     loads[SIGNAL].wait()
     signal_out_buf[...] = signal_ref[...].astype(F32).T.reshape(count, own, rows)
-    over_peers(send_signal)
+    pl.semaphore_wait(barrier, count - 1)
+
+    def near_seq(ring):
+        return upper * half_seqs + ring
+
+    def far_seq(ring):
+        return (1 - upper) * half_seqs + ring
+
+    def far_block(shift, to_group, ring):
+        to_seq = far_seq(ring)
+        place = to_group * seqs + to_seq
+
+        @pl.when(upper == 0)
+        def _():
+            transfer(signal_out_buf.at[place], signal_in.at[me], CROSS, to_group, to_seq).start()
+
+        @pl.when(upper == 1)
+        def _():
+            transfer(grad_out_buf.at[place], grad_in.at[me], CROSS, to_group, to_seq).start()
+
+    def far_taps(shift, to_group, ring):
+        if shift == 0:
+            place = group * seqs + far_seq(ring)
+            transfer(tap_out_buf.at[place], tap_in.at[seq], TAPS, group, far_seq(ring)).start()
+
+    def near_taps(shift, to_group, ring):
+        if shift == 0:
+            place = group * seqs + near_seq(ring)
+            transfer(tap_out_buf.at[place], tap_in.at[seq], TAPS, group, near_seq(ring)).start()
+
+    def near_grad_block(shift, to_group, ring):
+        place = to_group * seqs + near_seq(ring)
+        transfer(grad_out_buf.at[place], grad_in.at[me], GRAD, to_group, near_seq(ring)).start()
+
+    def near_signal_block(shift, to_group, ring):
+        place = to_group * seqs + near_seq(ring)
+        transfer(signal_out_buf.at[place], signal_in.at[me], SIGNAL, to_group, near_seq(ring)).start()
+
+    def mate_blocks(shift, to_group, ring):
+        place, to_seq = to_group * seqs + far_seq(ring), near_seq(ring)
+        transfer(grad_out_buf.at[place], near_grad_in.at[slot], NEAR_GRAD, to_group, to_seq).start()
+        transfer(signal_out_buf.at[place], near_signal_in.at[slot], NEAR_SIGNAL, to_group, to_seq).start()
+
+    def mate_taps(shift, to_group, ring):
+        place, to_seq = group * seqs + far_seq(ring), near_seq(ring)
+        if shift == 0:
+
+            @pl.when(upper == 0)
+            def _():
+                transfer(tap_out_buf.at[place], near_tap_in.at[inner], NEAR_TAPS, group, to_seq).start()
+
+    def in_turn(*sends):
+        for shift in shifts:
+            to_group = lax.rem(group + shift, groups) if shift else group
+            for offset in reversed(range(half_seqs)):
+                ring = lax.rem(inner + offset, half_seqs) if offset else inner
+                for send in sends:
+                    if shift or offset or send in (far_block, far_taps):
+                        send(shift, to_group, ring)
+
+    in_turn(far_taps, near_taps, mate_taps)
+    in_turn(mate_blocks)
+    in_turn(far_block, near_grad_block)
+    in_turn(near_signal_block)
     grad_in[me] = grad_out_buf[me]
     tap_in[seq] = tap_out_buf[me]
     signal_in[me] = signal_out_buf[me]
+    near_grad_in[slot] = grad_out_buf[group * seqs + mate]
+    near_signal_in[slot] = signal_out_buf[group * seqs + mate]
+    near_tap_in[inner] = tap_out_buf[group * seqs + mate]
 
     def spread(blocks, target, first_row):
         place = pl.ds(first_row, own)
         for k, (real, imag) in enumerate(coarse_forward(blocks)):
-            real, imag = turn(real, imag, cos_ref[k], sin_ref[k])
+            row = k * (seqs // len(blocks))
+            real, imag = turn(real, imag, cos_ref[row], sin_ref[row])
             target[k, place, re] = real
             target[k, place, im] = imag
 
@@ -213,23 +278,85 @@
         total = product(high, high_ref[...]) + product(low, high_ref[...]) + product(high, low_ref[...])
         target[...] = total.reshape(target.shape)
 
-    def collect(source, first_row):
-        place = pl.ds(first_row, own)
+    def collect(source, first_row, pieces):
+        place, stride = pl.ds(first_row, own), seqs // pieces
         terms = [
-            turn(source[k, place, re], source[k, place, im], cos_ref[k], sin_ref[k])
-            for k in range(coarse)
+            turn(source[k, place, re], source[k, place, im], cos_ref[k * stride], sin_ref[k * stride])
+            for k in range(pieces + 1)
         ]
-        return coarse_inverse(terms, scale)
+        return coarse_inverse(terms, 1.0 / (2 * pieces * rows))
 
     def row_of(index):
         return pl.multiple_of(index * own, own)
 
     for copy in loads[3:]:
         copy.wait()
+    all_of(near_grad_in, near_count - 1, NEAR_GRAD).wait_recv()
+    all_of(near_signal_in, near_count - 1, NEAR_SIGNAL).wait_recv()
+
+    def spread_near(index, carry):
+        for source, target in ((near_grad_in, near_grad), (near_signal_in, near_signal)):
+            spread([source[index * half_seqs + s] for s in range(half_seqs)], target, row_of(index))
+        return carry
+
+    lax.fori_loop(0, groups, spread_near, 0)
+    fine(near_grad, near_grad)
+    fine(near_signal, near_signal)
+    for k in range(half_seqs + 1):
+        real, imag = None, None
+        for index in range(groups):
+            place = pl.ds(index * own, own)
+            grad_re, grad_im = near_grad[k, place, re], near_grad[k, place, im]
+            signal_re, signal_im = near_signal[k, place, re], near_signal[k, place, im]
+            real = added(real, grad_re * signal_re + grad_im * signal_im)
+            imag = added(imag, grad_re * signal_im - grad_im * signal_re)
+        near_filter[k, :, re] = real
+        near_filter[k, :, im] = imag
+    fine(near_filter, near_filter)
+    for s, block in enumerate(collect(near_filter, 0, half_seqs)):
+        near_filter_out[s] = block
+    transfer(near_filter_out, part_in, PART, group, mate).start()
+
+    @pl.when(upper == 0)
+    def _():
+        all_of(near_tap_in, half_seqs - 1, NEAR_TAPS).wait_recv()
+        spread([near_tap_in[s] for s in range(half_seqs)], near_tap, 0)
+        fine(near_tap, near_tap)
+
+        def multiply_near(index, carry):
+            place = pl.ds(row_of(index), own)
+            for k in range(half_seqs + 1):
+                grad_re, grad_im = near_grad[k, place, re], near_grad[k, place, im]
+                tap_re, tap_im = near_tap[k, :, re], near_tap[k, :, im]
+                near_lines[k, place, re] = grad_re * tap_re + grad_im * tap_im
+                near_lines[k, place, im] = grad_re * tap_im - grad_im * tap_re
+            return carry
+
+        lax.fori_loop(0, groups, multiply_near, 0)
+        fine(near_lines, near_lines)
+
+        def collect_near(index, carry):
+            for s, block in enumerate(collect(near_lines, row_of(index), half_seqs)):
+                near_input_out[index * half_seqs + s] = block
+            return carry
+
+        lax.fori_loop(0, groups, collect_near, 0)
+        for shift in shifts:
+            to_group = lax.rem(group + shift, groups) if shift else group
+            for offset in reversed(range(half_seqs)):
+                if shift or offset:
+                    ring = lax.rem(inner + offset, half_seqs)
+                    transfer(
+                        near_input_out.at[to_group * half_seqs + ring], near_input_in.at[slot],
+                        NEAR_INPUT, to_group, ring,
+                    ).start()
+        near_input_in[slot] = near_input_out[slot]
+
     all_of(tap_in, seqs - 1, TAPS).wait_recv()
     spread([tap_in[s] for s in range(seqs)], tap_rows, 0)
     fine(tap_rows, tap_spec)
-    all_of(grad_in, count - 1, GRAD).wait_recv()
+    all_of(grad_in, near_count - 1, GRAD).wait_recv()
+    pl.when(upper == 0)(lambda: all_of(grad_in, near_count, CROSS).wait_recv())
 
     def group_at(index):
         return lax.rem(2 * pair + index, groups)
@@ -259,7 +386,7 @@
 
         def collect_input(index, carry):
             here = group_at(2 * first + index)
-            for s, block in enumerate(collect(lines, row_of(index))):
+            for s, block in enumerate(collect(lines, row_of(index), seqs)):
                 input_out[here * seqs + s] = block
             return carry
 
@@ -277,7 +404,8 @@
         input_part(first)
     input_in[me] = input_out[me]
 
-    all_of(signal_in, count - 1, SIGNAL).wait_recv()
+    all_of(signal_in, near_count - 1, SIGNAL).wait_recv()
+    pl.when(upper == 1)(lambda: all_of(signal_in, near_count, CROSS).wait_recv())
 
     def spread_signal(index, carry):
         here = group_at(index)
@@ -298,8 +426,9 @@
         filter_rows[k, :, re] = real
         filter_rows[k, :, im] = imag
     fine(filter_rows, filter_spec)
-    for s, block in enumerate(collect(filter_spec, 0)):
-        filter_out[s] = block
+    all_of(part_in, half_seqs, PART).wait_recv()
+    for s, block in enumerate(collect(filter_spec, 0, seqs)):
+        filter_out[s] = block + part_in[s] if s < half_seqs else block
 
     for offset in turns:
         for flip in range(half_groups):
@@ -313,6 +442,14 @@
 
     half = count // 2
     all_of(input_in, count - 1, INPUT).wait_recv()
+
+    @pl.when(upper == 0)
+    def _():
+        all_of(near_input_in, near_count - 1, NEAR_INPUT).wait_recv()
+        for where in range(groups):
+            far = slice(where * seqs + half_seqs, (where + 1) * seqs)
+            input_in[far] = input_in[far] + near_input_in[where * half_seqs : (where + 1) * half_seqs]
+
     gradient = input_in[...].reshape(channels, rows).T + skip_ref[...] * grad_ref[...].astype(F32)
     input_ref[...] = gradient.astype(BF16)
     all_of(filter_in.at[0], half - 1, FILTER).wait_recv()
@@ -321,8 +458,17 @@
     forward = transfer(mine, mine, FORWARD, partner, seq)
     forward.start()
     forward.wait_recv()
-    for kind, buffer in ((GRAD, grad_in), (SIGNAL, signal_in), (INPUT, input_in)):
-        all_of(buffer, count - 1, kind).wait_send()
+    for kind in (GRAD, SIGNAL, NEAR_GRAD, NEAR_SIGNAL):
+        all_of(grad_in, near_count - 1, kind).wait_send()
+    all_of(grad_in, near_count, CROSS).wait_send()
+    all_of(part_in, half_seqs, PART).wait_send()
+
+    @pl.when(upper == 0)
+    def _():
+        all_of(grad_in, near_count - 1, NEAR_INPUT).wait_send()
+        all_of(tap_in, half_seqs - 1, NEAR_TAPS).wait_send()
+
+    all_of(input_in, count - 1, INPUT).wait_send()
     all_of(filter_in.at[0], half - 1, FILTER).wait_send()
     forward.wait_send()
     all_of(tap_in, seqs - 1, TAPS).wait_send()
@@ -366,6 +512,9 @@
     cos_turn, sin_turn = turn_tables(seqs, rows, own)
     blocks = pltpu.VMEM((count, own, rows), F32)
     few = pltpu.VMEM((seqs, own, rows), F32)
+    half_blocks = pltpu.VMEM((count // 2, own, rows), F32)
+    half_few = pltpu.VMEM((seqs // 2, own, rows), F32)
+    near = lambda number: pltpu.VMEM((seqs // 2 + 1, number * own, 2 * rows), F32)
     lines = lambda number: pltpu.VMEM((coarse, number * own, 2 * rows), F32)
     pairs = pltpu.VMEM((groups // 2, coarse, 2 * own, 2 * rows), F32)
     hbm = pl.BlockSpec(memory_space=pltpu.HBM)
@@ -388,8 +537,10 @@
             blocks, few, blocks,
             lines(1), lines(1), pairs, pairs, lines(groups), lines(groups),
             pairs, lines(1), lines(1),
-            pltpu.SemaphoreType.DMA((6,)),
-            pltpu.SemaphoreType.DMA((6,)),
+            half_blocks, half_blocks, half_few, half_blocks, half_blocks, half_few, half_few,
+            near(groups), near(groups), near(1), near(groups), near(1),
+            pltpu.SemaphoreType.DMA((12,)),
+            pltpu.SemaphoreType.DMA((12,)),
             pltpu.SemaphoreType.DMA((8,)),
         ],
         compiler_params=pltpu.CompilerParams(
@@ -425,7 +576,7 @@
     rows, channels = filter_taps.shape
     return (
         signal.shape[0] == 1
-        and seqs % 2 == 0
+        and seqs % 4 == 0
         and groups % 2 == 0
         and rows % 128 == 0
         and channels % (8 * groups * seqs) == 0

time: 31.9 us -> 30.6 us (0.959)
  Pallas kernels: 31.1 us -> 29.8 us
    pallas_call x1, Pallas kernels: 30.3 us -> 29 us  [fused_shards(): pl.pallas_call(functools.partial(fused_kernel, groups, seqs), out_shape=(...]
where the time goes in v4:
time: 30.6 us; the launch traced here: 30.5 us
  Pallas kernels  29.8 us (97%)
  between operations  0.64 us (2%)
    pallas_call x1, Pallas kernels, fused_shards(): pl.pallas_call(functools.partial(fused_kernel, groups, seqs), out_shape=(...  29 us
    pallas_call x1, Pallas kernels, fused_shards(): pl.pallas_call(functools.partial(finish_kernel, groups, seqs), out_shape=...  0.86 us

profile of v4, /device:TPU:0, one launch (start us, length us, event | category | flops | bytes accessed | tf_op | source)
XLA Modules:
  0.0 30.5 jit_solution(14355769911052849878)
XLA Ops:
  0.6 29.0 %shard_map.95 = (bf16[256,256]{1,0:T(8,128)(2,1)S(1)}, f32[2,16,8,256]{3,2,1,0:T(8,128)S(1)}) custom-call(bf16[256,256]{1,0:T(8,128)(2,1)} %bitcast.4, bf16[256,256]{1,0:T(8,128)(2,1)} %bitcast.5, f32[256,256]{1,0:T(8,128)} %tap_hbm.1, f32[1,256]{1,0:T(1,128)} %bitcast.6, bf16[512,512]{1,0:T(8,128)(2,1)} %constant.8.clone.high_hbm, ...), custom_call_target="tpu_custom_call" | custom-call | tf_op jit(solution)/shard_map/pallas_call | solution.py:524
  29.6 0.9 %shard_map.96 = (bf16[256,256]{1,0:T(8,128)(2,1)}, f32[256,256]{1,0:T(8,128)}) custom-call(bf16[256,256]{1,0:T(8,128)(2,1)S(1)} %get-tuple-element.6.input_ref, f32[2,16,8,256]{3,2,1,0:T(8,128)S(1)} %get-tuple-element.7.filter_in), custom_call_target="tpu_custom_call" | custom-call | tf_op jit(solution)/shard_map/pallas_call | solution.py:558

commit v5 on v4

--- a/solution.py
+++ b/solution.py
@@ -291,6 +291,16 @@
 
     for copy in loads[3:]:
         copy.wait()
+    all_of(tap_in, seqs - 1, TAPS).wait_recv()
+    spread([tap_in[s] for s in range(seqs)], tap_rows, 0)
+    fine(tap_rows, tap_spec)
+
+    @pl.when(upper == 0)
+    def _():
+        all_of(near_tap_in, half_seqs - 1, NEAR_TAPS).wait_recv()
+        spread([near_tap_in[s] for s in range(half_seqs)], near_tap, 0)
+        fine(near_tap, near_tap)
+
     all_of(near_grad_in, near_count - 1, NEAR_GRAD).wait_recv()
     all_of(near_signal_in, near_count - 1, NEAR_SIGNAL).wait_recv()
 
@@ -319,10 +329,6 @@
 
     @pl.when(upper == 0)
     def _():
-        all_of(near_tap_in, half_seqs - 1, NEAR_TAPS).wait_recv()
-        spread([near_tap_in[s] for s in range(half_seqs)], near_tap, 0)
-        fine(near_tap, near_tap)
-
         def multiply_near(index, carry):
             place = pl.ds(row_of(index), own)
             for k in range(half_seqs + 1):
@@ -352,9 +358,6 @@
                     ).start()
         near_input_in[slot] = near_input_out[slot]
 
-    all_of(tap_in, seqs - 1, TAPS).wait_recv()
-    spread([tap_in[s] for s in range(seqs)], tap_rows, 0)
-    fine(tap_rows, tap_spec)
     all_of(grad_in, near_count - 1, GRAD).wait_recv()
     pl.when(upper == 0)(lambda: all_of(grad_in, near_count, CROSS).wait_recv())
 
@@ -369,8 +372,9 @@
             spread([grad_in[here * seqs + s] for s in range(seqs)], source, row_of(index))
             return carry
 
-        lax.fori_loop(0, 2, spread_grad, 0)
-        fine(source, spectrum)
+        def transform():
+            lax.fori_loop(0, 2, spread_grad, 0)
+            fine(source, spectrum)
 
         def multiply_taps(index, carry):
             place = pl.ds(row_of(index), own)
@@ -381,28 +385,32 @@
                 lines[k, place, im] = grad_re * tap_im - grad_im * tap_re
             return carry
 
-        lax.fori_loop(0, 2, multiply_taps, 0)
-        fine(lines, lines)
-
         def collect_input(index, carry):
             here = group_at(2 * first + index)
             for s, block in enumerate(collect(lines, row_of(index), seqs)):
                 input_out[here * seqs + s] = block
             return carry
 
-        lax.fori_loop(0, 2, collect_input, 0)
-
-        for offset in turns:
-            for flip in range(2):
-                if first or offset or flip:
-                    to_group = group_at(2 * first + lax.rem(parity + flip, 2))
-                    to_seq = turned_seq(offset)
-                    place = to_group * seqs + to_seq
-                    transfer(input_out.at[place], input_in.at[me], INPUT, to_group, to_seq).start()
-
-    for first in reversed(range(half_groups)):
-        input_part(first)
-    input_in[me] = input_out[me]
+        def finish():
+            lax.fori_loop(0, 2, multiply_taps, 0)
+            fine(lines, lines)
+            lax.fori_loop(0, 2, collect_input, 0)
+
+            for offset in turns:
+                for flip in range(2):
+                    if first or offset or flip:
+                        to_group = group_at(2 * first + lax.rem(parity + flip, 2))
+                        to_seq = turned_seq(offset)
+                        place = to_group * seqs + to_seq
+                        transfer(input_out.at[place], input_in.at[me], INPUT, to_group, to_seq).start()
+
+        return transform, finish
+
+    parts = [input_part(first) for first in reversed(range(half_groups))]
+    parts[0][0]()
+    parts[0][1]()
+    for transform, _ in parts[1:]:
+        transform()
 
     all_of(signal_in, near_count - 1, SIGNAL).wait_recv()
     pl.when(upper == 1)(lambda: all_of(signal_in, near_count, CROSS).wait_recv())
@@ -438,9 +446,17 @@
                 transfer(
                     filter_out.at[to_seq], filter_in.at[parity, pair * seqs + seq], FILTER, to_group, to_seq
                 ).start()
+    for _, finish in parts[1:]:
+        finish()
+    input_in[me] = input_out[me]
     filter_in[parity, pair * seqs + seq] = filter_out[seq]
 
     half = count // 2
+    all_of(filter_in.at[0], half - 1, FILTER).wait_recv()
+    mine = filter_in.at[parity]
+    partner = 2 * pair + 1 - parity
+    forward = transfer(mine, mine, FORWARD, partner, seq)
+    forward.start()
     all_of(input_in, count - 1, INPUT).wait_recv()
 
     @pl.when(upper == 0)
@@ -452,11 +468,6 @@
 
     gradient = input_in[...].reshape(channels, rows).T + skip_ref[...] * grad_ref[...].astype(F32)
     input_ref[...] = gradient.astype(BF16)
-    all_of(filter_in.at[0], half - 1, FILTER).wait_recv()
-    mine = filter_in.at[parity]
-    partner = 2 * pair + 1 - parity
-    forward = transfer(mine, mine, FORWARD, partner, seq)
-    forward.start()
     forward.wait_recv()
     for kind in (GRAD, SIGNAL, NEAR_GRAD, NEAR_SIGNAL):
         all_of(grad_in, near_count - 1, kind).wait_send()

time: 30.6 us -> 29.8 us (0.974)
  Pallas kernels: 29.8 us -> 29 us
    pallas_call x1, Pallas kernels: 29 us -> 28.2 us  [fused_shards(): pl.pallas_call(functools.partial(fused_kernel, groups, seqs), out_shape=(...]
where the time goes in v5:
time: 29.8 us; the launch traced here: 29.7 us
  Pallas kernels  29 us (97%)
  between operations  0.64 us (2%)
    pallas_call x1, Pallas kernels, fused_shards(): pl.pallas_call(functools.partial(fused_kernel, groups, seqs), out_shape=(...  28.2 us
    pallas_call x1, Pallas kernels, fused_shards(): pl.pallas_call(functools.partial(finish_kernel, groups, seqs), out_shape=...  0.86 us

profile of v5, /device:TPU:0, one launch (start us, length us, event | category | flops | bytes accessed | tf_op | source)
XLA Modules:
  0.0 29.7 jit_solution(5282405172296896421)
XLA Ops:
  0.6 28.2 %shard_map.95 = (bf16[256,256]{1,0:T(8,128)(2,1)S(1)}, f32[2,16,8,256]{3,2,1,0:T(8,128)S(1)}) custom-call(bf16[256,256]{1,0:T(8,128)(2,1)} %bitcast.4, bf16[256,256]{1,0:T(8,128)(2,1)} %bitcast.5, f32[256,256]{1,0:T(8,128)} %tap_hbm.1, f32[1,256]{1,0:T(1,128)} %bitcast.6, bf16[512,512]{1,0:T(8,128)(2,1)} %constant.8.clone.high_hbm, ...), custom_call_target="tpu_custom_call" | custom-call | tf_op jit(solution)/shard_map/pallas_call | solution.py:535
  28.8 0.9 %shard_map.96 = (bf16[256,256]{1,0:T(8,128)(2,1)}, f32[256,256]{1,0:T(8,128)}) custom-call(bf16[256,256]{1,0:T(8,128)(2,1)S(1)} %get-tuple-element.6.input_ref, f32[2,16,8,256]{3,2,1,0:T(8,128)S(1)} %get-tuple-element.7.filter_in), custom_call_target="tpu_custom_call" | custom-call | tf_op jit(solution)/shard_map/pallas_call | solution.py:569

commit v6 on v5

--- a/solution.py
+++ b/solution.py
@@ -12,7 +12,7 @@
 MESH = pl.DeviceIdType.MESH
 F32 = jnp.float32
 BF16 = jnp.bfloat16
-GRAD, TAPS, SIGNAL, INPUT, FILTER, FORWARD, CROSS, NEAR_GRAD, NEAR_SIGNAL, NEAR_TAPS, PART, NEAR_INPUT = range(12)
+GRAD, TAPS, SIGNAL, INPUT, FILTER, FORWARD, CROSS, NEAR_GRAD, NEAR_SIGNAL, NEAR_TAPS, PART, NEAR_INPUT, CROSS_OWN = range(13)
 
 
 def weighted(terms):
@@ -199,16 +199,16 @@
         return (1 - upper) * half_seqs + ring
 
     def far_block(shift, to_group, ring):
-        to_seq = far_seq(ring)
+        to_seq, kind = far_seq(ring), CROSS if shift >= 2 else CROSS_OWN
         place = to_group * seqs + to_seq
 
         @pl.when(upper == 0)
         def _():
-            transfer(signal_out_buf.at[place], signal_in.at[me], CROSS, to_group, to_seq).start()
+            transfer(signal_out_buf.at[place], signal_in.at[me], kind, to_group, to_seq).start()
 
         @pl.when(upper == 1)
         def _():
-            transfer(grad_out_buf.at[place], grad_in.at[me], CROSS, to_group, to_seq).start()
+            transfer(grad_out_buf.at[place], grad_in.at[me], kind, to_group, to_seq).start()
 
     def far_taps(shift, to_group, ring):
         if shift == 0:
@@ -242,8 +242,8 @@
                 transfer(tap_out_buf.at[place], near_tap_in.at[inner], NEAR_TAPS, group, to_seq).start()
 
     def in_turn(*sends):
-        for shift in shifts:
-            to_group = lax.rem(group + shift, groups) if shift else group
+        for shift in (*range(2, groups), 1, 0):
+            to_group = 2 * lax.rem(pair + shift // 2, half_groups) + lax.rem(parity + shift, 2)
             for offset in reversed(range(half_seqs)):
                 ring = lax.rem(inner + offset, half_seqs) if offset else inner
                 for send in sends:
@@ -359,7 +359,9 @@
         near_input_in[slot] = near_input_out[slot]
 
     all_of(grad_in, near_count - 1, GRAD).wait_recv()
-    pl.when(upper == 0)(lambda: all_of(grad_in, near_count, CROSS).wait_recv())
+    own_far = 2 * half_seqs
+    other_far = near_count - own_far
+    pl.when(upper == 0)(lambda: all_of(grad_in, other_far, CROSS).wait_recv())
 
     def group_at(index):
         return lax.rem(2 * pair + index, groups)
@@ -409,11 +411,17 @@
     parts = [input_part(first) for first in reversed(range(half_groups))]
     parts[0][0]()
     parts[0][1]()
+    pl.when(upper == 0)(lambda: all_of(grad_in, own_far, CROSS_OWN).wait_recv())
     for transform, _ in parts[1:]:
         transform()
 
     all_of(signal_in, near_count - 1, SIGNAL).wait_recv()
-    pl.when(upper == 1)(lambda: all_of(signal_in, near_count, CROSS).wait_recv())
+
+    @pl.when(upper == 1)
+    def _():
+        all_of(signal_in, other_far, CROSS).wait_recv()
+        all_of(signal_in, own_far, CROSS_OWN).wait_recv()
+
 
     def spread_signal(index, carry):
         here = group_at(index)
@@ -471,7 +479,8 @@
     forward.wait_recv()
     for kind in (GRAD, SIGNAL, NEAR_GRAD, NEAR_SIGNAL):
         all_of(grad_in, near_count - 1, kind).wait_send()
-    all_of(grad_in, near_count, CROSS).wait_send()
+    all_of(grad_in, other_far, CROSS).wait_send()
+    all_of(grad_in, own_far, CROSS_OWN).wait_send()
     all_of(part_in, half_seqs, PART).wait_send()
 
     @pl.when(upper == 0)
@@ -550,8 +559,8 @@
             pairs, lines(1), lines(1),
             half_blocks, half_blocks, half_few, half_blocks, half_blocks, half_few, half_few,
             near(groups), near(groups), near(1), near(groups), near(1),
-            pltpu.SemaphoreType.DMA((12,)),
-            pltpu.SemaphoreType.DMA((12,)),
+            pltpu.SemaphoreType.DMA((13,)),
+            pltpu.SemaphoreType.DMA((13,)),
             pltpu.SemaphoreType.DMA((8,)),
         ],
         compiler_params=pltpu.CompilerParams(
@@ -589,6 +598,7 @@
         signal.shape[0] == 1
         and seqs % 4 == 0
         and groups % 2 == 0
+        and groups > 2
         and rows % 128 == 0
         and channels % (8 * groups * seqs) == 0
     )

time: 29.8 us -> 29.6 us (level)
  no operation moved by 1% of the time
where the time goes in v6:
time: 29.6 us; the launch traced here: 29.4 us
  Pallas kernels  28.8 us (97%)
  between operations  0.64 us (2%)
    pallas_call x1, Pallas kernels, fused_shards(): pl.pallas_call(functools.partial(fused_kernel, groups, seqs), out_shape=(...  27.9 us
    pallas_call x1, Pallas kernels, fused_shards(): pl.pallas_call(functools.partial(finish_kernel, groups, seqs), out_shape=...  0.86 us

profile of v6, /device:TPU:0, one launch (start us, length us, event | category | flops | bytes accessed | tf_op | source)
XLA Modules:
  0.0 29.4 jit_solution(8263719331058270704)
XLA Ops:
  0.6 27.9 %shard_map.95 = (bf16[256,256]{1,0:T(8,128)(2,1)S(1)}, f32[2,16,8,256]{3,2,1,0:T(8,128)S(1)}) custom-call(bf16[256,256]{1,0:T(8,128)(2,1)} %bitcast.4, bf16[256,256]{1,0:T(8,128)(2,1)} %bitcast.5, f32[256,256]{1,0:T(8,128)} %tap_hbm.1, f32[1,256]{1,0:T(1,128)} %bitcast.6, bf16[512,512]{1,0:T(8,128)(2,1)} %constant.8.clone.high_hbm, ...), custom_call_target="tpu_custom_call" | custom-call | tf_op jit(solution)/shard_map/pallas_call | solution.py:544
  28.6 0.9 %shard_map.96 = (bf16[256,256]{1,0:T(8,128)(2,1)}, f32[256,256]{1,0:T(8,128)}) custom-call(bf16[256,256]{1,0:T(8,128)(2,1)S(1)} %get-tuple-element.6.input_ref, f32[2,16,8,256]{3,2,1,0:T(8,128)S(1)} %get-tuple-element.7.filter_in), custom_call_target="tpu_custom_call" | custom-call | tf_op jit(solution)/shard_map/pallas_call | solution.py:578

commit v7 on v6

--- a/solution.py
+++ b/solution.py
@@ -327,6 +327,60 @@
         near_filter_out[s] = block
     transfer(near_filter_out, part_in, PART, group, mate).start()
 
+    all_of(grad_in, near_count - 1, GRAD).wait_recv()
+    own_far = 2 * half_seqs
+    other_far = near_count - own_far
+    pl.when(upper == 0)(lambda: all_of(grad_in, other_far, CROSS).wait_recv())
+
+    def group_at(index):
+        return lax.rem(2 * pair + index, groups)
+
+    def input_part(first):
+        source, spectrum, lines = grad_rows.at[first], grad_spec.at[first], input_rows.at[first]
+
+        def spread_grad(index, carry):
+            here = group_at(2 * first + index)
+            spread([grad_in[here * seqs + s] for s in range(seqs)], source, row_of(index))
+            return carry
+
+        def transform():
+            lax.fori_loop(0, 2, spread_grad, 0)
+            fine(source, spectrum)
+
+        def multiply_taps(index, carry):
+            place = pl.ds(row_of(index), own)
+            for k in range(coarse):
+                grad_re, grad_im = spectrum[k, place, re], spectrum[k, place, im]
+                tap_re, tap_im = tap_spec[k, :, re], tap_spec[k, :, im]
+                lines[k, place, re] = grad_re * tap_re + grad_im * tap_im
+                lines[k, place, im] = grad_re * tap_im - grad_im * tap_re
+            return carry
+
+        def collect_input(index, carry):
+            here = group_at(2 * first + index)
+            for s, block in enumerate(collect(lines, row_of(index), seqs)):
+                input_out[here * seqs + s] = block
+            return carry
+
+        def finish():
+            lax.fori_loop(0, 2, multiply_taps, 0)
+            fine(lines, lines)
+            lax.fori_loop(0, 2, collect_input, 0)
+
+            for offset in turns:
+                for flip in range(2):
+                    if first or offset or flip:
+                        to_group = group_at(2 * first + lax.rem(parity + flip, 2))
+                        to_seq = turned_seq(offset)
+                        place = to_group * seqs + to_seq
+                        transfer(input_out.at[place], input_in.at[me], INPUT, to_group, to_seq).start()
+
+        return transform, finish
+
+    parts = [input_part(first) for first in reversed(range(half_groups))]
+    parts[0][0]()
+    parts[0][1]()
+
     @pl.when(upper == 0)
     def _():
         def multiply_near(index, carry):
@@ -358,59 +412,6 @@
                     ).start()
         near_input_in[slot] = near_input_out[slot]
 
-    all_of(grad_in, near_count - 1, GRAD).wait_recv()
-    own_far = 2 * half_seqs
-    other_far = near_count - own_far
-    pl.when(upper == 0)(lambda: all_of(grad_in, other_far, CROSS).wait_recv())
-
-    def group_at(index):
-        return lax.rem(2 * pair + index, groups)
-
-    def input_part(first):
-        source, spectrum, lines = grad_rows.at[first], grad_spec.at[first], input_rows.at[first]
-
-        def spread_grad(index, carry):
-            here = group_at(2 * first + index)
-            spread([grad_in[here * seqs + s] for s in range(seqs)], source, row_of(index))
-            return carry
-
-        def transform():
-            lax.fori_loop(0, 2, spread_grad, 0)
-            fine(source, spectrum)
-
-        def multiply_taps(index, carry):
-            place = pl.ds(row_of(index), own)
-            for k in range(coarse):
-                grad_re, grad_im = spectrum[k, place, re], spectrum[k, place, im]
-                tap_re, tap_im = tap_spec[k, :, re], tap_spec[k, :, im]
-                lines[k, place, re] = grad_re * tap_re + grad_im * tap_im
-                lines[k, place, im] = grad_re * tap_im - grad_im * tap_re
-            return carry
-
-        def collect_input(index, carry):
-            here = group_at(2 * first + index)
-            for s, block in enumerate(collect(lines, row_of(index), seqs)):
-                input_out[here * seqs + s] = block
-            return carry
-
-        def finish():
-            lax.fori_loop(0, 2, multiply_taps, 0)
-            fine(lines, lines)
-            lax.fori_loop(0, 2, collect_input, 0)
-
-            for offset in turns:
-                for flip in range(2):
-                    if first or offset or flip:
-                        to_group = group_at(2 * first + lax.rem(parity + flip, 2))
-                        to_seq = turned_seq(offset)
-                        place = to_group * seqs + to_seq
-                        transfer(input_out.at[place], input_in.at[me], INPUT, to_group, to_seq).start()
-
-        return transform, finish
-
-    parts = [input_part(first) for first in reversed(range(half_groups))]
-    parts[0][0]()
-    parts[0][1]()
     pl.when(upper == 0)(lambda: all_of(grad_in, own_far, CROSS_OWN).wait_recv())
     for transform, _ in parts[1:]:
         transform()

time: 29.6 us -> 30 us (1.014)
  Pallas kernels: 28.8 us -> 29.2 us
    pallas_call x1, Pallas kernels: 27.9 us -> 28.4 us  [fused_shards(): pl.pallas_call(functools.partial(fused_kernel, groups, seqs), out_shape=(...]
where the time goes in v7:
time: 30 us; the launch traced here: 29.9 us
  Pallas kernels  29.2 us (97%)
  between operations  0.64 us (2%)
    pallas_call x1, Pallas kernels, fused_shards(): pl.pallas_call(functools.partial(fused_kernel, groups, seqs), out_shape=(...  28.4 us
    pallas_call x1, Pallas kernels, fused_shards(): pl.pallas_call(functools.partial(finish_kernel, groups, seqs), out_shape=...  0.86 us

profile of v7, /device:TPU:0, one launch (start us, length us, event | category | flops | bytes accessed | tf_op | source)
XLA Modules:
  0.0 29.9 jit_solution(15734347905387547051)
XLA Ops:
  0.6 28.4 %shard_map.95 = (bf16[256,256]{1,0:T(8,128)(2,1)S(1)}, f32[2,16,8,256]{3,2,1,0:T(8,128)S(1)}) custom-call(bf16[256,256]{1,0:T(8,128)(2,1)} %bitcast.4, bf16[256,256]{1,0:T(8,128)(2,1)} %bitcast.5, f32[256,256]{1,0:T(8,128)} %tap_hbm.1, f32[1,256]{1,0:T(1,128)} %bitcast.6, bf16[512,512]{1,0:T(8,128)(2,1)} %constant.8.clone.high_hbm, ...), custom_call_target="tpu_custom_call" | custom-call | tf_op jit(solution)/shard_map/pallas_call | solution.py:545
  29.0 0.9 %shard_map.96 = (bf16[256,256]{1,0:T(8,128)(2,1)}, f32[256,256]{1,0:T(8,128)}) custom-call(bf16[256,256]{1,0:T(8,128)(2,1)S(1)} %get-tuple-element.6.input_ref, f32[2,16,8,256]{3,2,1,0:T(8,128)S(1)} %get-tuple-element.7.filter_in), custom_call_target="tpu_custom_call" | custom-call | tf_op jit(solution)/shard_map/pallas_call | solution.py:579
